TPU v7x, 32 devices: a whole 2x2x4 slice. The times are simulated.
32 devices in a mesh: data: 2 (over x), model: 4 (over z), beam: 4 (over y, core).
Axes of the slice: x: 2, y: 2, z: 4, core: 2. Of those that a mesh axis runs over, the one named last changes fastest.
Arguments:
- x_embed: bfloat16 [128, 1024], P(('data', 'beam')), parts along dimension 0
- parent: int32 [4, 32], P('data'), parts along dimension 0
- position: int32 [], replicated
- score: float32 [128], P(('data', 'beam')), parts along dimension 0
- k_cache: bfloat16 [4, 128, 256, 16, 64], P(None, ('data', 'beam'), None, 'model'), parts along dimension 1
- v_cache: bfloat16 [4, 128, 256, 16, 64], P(None, ('data', 'beam'), None, 'model'), parts along dimension 1
- gain_attn: bfloat16 [4, 1024], replicated
- w_query: bfloat16 [4, 1024, 1024], P(None, None, 'model')
- w_key: bfloat16 [4, 1024, 1024], P(None, None, 'model')
- w_value: bfloat16 [4, 1024, 1024], P(None, None, 'model')
- w_out: bfloat16 [4, 1024, 1024], P(None, 'model')
- gain_mlp: bfloat16 [4, 1024], replicated
- w_gate: bfloat16 [4, 1024, 4096], P(None, None, 'model')
- w_up: bfloat16 [4, 1024, 4096], P(None, None, 'model')
- w_down: bfloat16 [4, 4096, 1024], P(None, 'model')
- gain_final: bfloat16 [1024], replicated
- w_vocab: bfloat16 [1024, 32128], P(None, 'model')
Outputs:
- output 1: bfloat16 [4, 128, 256, 16, 64], P(None, ('data', 'beam'), None, 'model'), parts along dimension 1
- output 2: bfloat16 [4, 128, 256, 16, 64], P(None, ('data', 'beam'), None, 'model'), parts along dimension 1
- output 3: float32 [128, 32128], P(('data', 'beam'), 'model'), parts along dimension 0
There are 2 independent parts. A program takes and returns all parts, laid end to end along the dimension named above; an argument that names none is the same for every part.
All inputs are finite; a program needn't handle non-finite values.
Results may differ from a plain program's by a relative error of at most 0.00139351.
Values are sent between devices in bfloat16 or wider.
A program may use at most 1 GiB of HBM per device.

v0:
```python
import jax
import jax.numpy as jnp
from jax import lax
from jax.sharding import PartitionSpec as P

NORM_EPS = 1e-6
ROPE_BASE = 10000.0


def rms_norm(residual, gain):
    inv_rms = lax.rsqrt(jnp.mean(residual * residual, axis=-1, keepdims=True) + NORM_EPS)
    return (residual * inv_rms * gain.astype(jnp.float32)).astype(jnp.bfloat16)


def rope_rotate(vectors, position):
    half_dim = vectors.shape[-1] // 2
    inv_freq = ROPE_BASE ** (-jnp.arange(half_dim, dtype=jnp.float32) / half_dim)
    angles = position.astype(jnp.float32) * inv_freq
    cos_part = jnp.cos(angles)
    sin_part = jnp.sin(angles)
    lower_half = vectors[..., :half_dim]
    upper_half = vectors[..., half_dim:]
    return jnp.concatenate([lower_half * cos_part - upper_half * sin_part, upper_half * cos_part + lower_half * sin_part], axis=-1)


def layer_body(residual, k_sel, v_sel, position, gain_attn, w_query, w_key, w_value, w_out, gain_mlp, w_gate, w_up, w_down):
    beam_rows, cache_len, kv_local, head_dim = k_sel.shape
    heads_local = w_query.shape[1] // head_dim
    group_size = heads_local // kv_local
    normed = rms_norm(residual, gain_attn)
    q_rot = rope_rotate(jnp.dot(normed, w_query, preferred_element_type=jnp.float32).reshape(beam_rows, heads_local, head_dim), position).astype(jnp.bfloat16)
    k_new = rope_rotate(jnp.dot(normed, w_key, preferred_element_type=jnp.float32).reshape(beam_rows, kv_local, head_dim), position).astype(jnp.bfloat16)
    v_new = jnp.dot(normed, w_value, preferred_element_type=jnp.float32).astype(jnp.bfloat16).reshape(beam_rows, kv_local, head_dim)
    k_sel = lax.dynamic_update_slice(k_sel, k_new[:, None], (0, position, 0, 0))
    v_sel = lax.dynamic_update_slice(v_sel, v_new[:, None], (0, position, 0, 0))
    slot_mask = (jnp.arange(cache_len) <= position)[None, None, None, :]
    q_grouped = q_rot.reshape(beam_rows, kv_local, group_size, head_dim)
    logits = jnp.einsum('bkgd,bskd->bkgs', q_grouped, k_sel, preferred_element_type=jnp.float32) * head_dim ** -0.5
    logits = jnp.where(slot_mask, logits, -jnp.inf)
    attn_prob = jax.nn.softmax(logits, axis=-1).astype(jnp.bfloat16)
    attn_out = jnp.einsum('bkgs,bskd->bkgd', attn_prob, v_sel, preferred_element_type=jnp.float32).astype(jnp.bfloat16)
    attn_part = jnp.dot(attn_out.reshape(beam_rows, heads_local * head_dim), w_out, preferred_element_type=jnp.float32)
    residual = residual + lax.psum(attn_part, 'model')
    normed = rms_norm(residual, gain_mlp)
    gate_proj = jnp.dot(normed, w_gate, preferred_element_type=jnp.float32)
    up_proj = jnp.dot(normed, w_up, preferred_element_type=jnp.float32)
    hidden = (jax.nn.silu(gate_proj) * up_proj).astype(jnp.bfloat16)
    residual = residual + lax.psum(jnp.dot(hidden, w_down, preferred_element_type=jnp.float32), 'model')
    return residual, k_sel, v_sel


def vocab_log_softmax(logits):
    local_max = jnp.max(logits, axis=-1, keepdims=True)
    global_max = lax.pmax(local_max, 'model')
    sum_exp = lax.psum(jnp.sum(jnp.exp(logits - global_max), axis=-1, keepdims=True), 'model')
    return logits - global_max - jnp.log(sum_exp)


def solution(mesh):
    beam_size = mesh.shape['beam']
    cache_spec = P(None, ('data', 'beam'), None, 'model', None)
    col_spec = P(None, None, 'model')
    row_spec = P(None, 'model', None)
    in_specs = (P(('data', 'beam'), None), P('data', None), P(), P(('data', 'beam')), cache_spec, cache_spec,
                P(), col_spec, col_spec, col_spec, row_spec, P(), col_spec, col_spec, row_spec, P(), P(None, 'model'))
    out_specs = (cache_spec, cache_spec, P(('data', 'beam'), 'model'))

    def local_step(x_embed, parent, position, score, k_cache, v_cache, gain_attn, w_query, w_key, w_value, w_out, gain_mlp, w_gate, w_up, w_down, gain_final, w_vocab):
        layers = k_cache.shape[0]
        beam_rows = x_embed.shape[0]
        sent_span = parent.shape[1] // beam_rows
        my_index = lax.axis_index('beam')
        block_start = (my_index // sent_span) * sent_span
        my_pos = my_index - block_start
        flat_parent = parent.reshape(-1)
        my_parent = lax.dynamic_slice(flat_parent, (my_index * beam_rows,), (beam_rows,))
        src_shift = (my_pos - (my_parent // beam_rows - block_start)) % sent_span
        pick_index = src_shift * beam_rows + jnp.where(src_shift == 0, my_parent % beam_rows, jnp.arange(beam_rows, dtype=jnp.int32))
        send_index = []
        permutations = []
        for shift_by in range(1, sent_span):
            partner = block_start + (my_pos + shift_by) % sent_span
            partner_parent = lax.dynamic_slice(flat_parent, (partner * beam_rows,), (beam_rows,))
            send_index.append(jnp.clip(partner_parent - my_index * beam_rows, 0, beam_rows - 1))
            permutations.append([(device_id, (device_id // sent_span) * sent_span + (device_id % sent_span + shift_by) % sent_span) for device_id in range(beam_size)])

        def reorder(cache_layer):
            pooled = [cache_layer]
            for step_idx in range(sent_span - 1):
                outgoing = jnp.take(cache_layer, send_index[step_idx], axis=0)
                pooled.append(lax.ppermute(outgoing, 'beam', permutations[step_idx]))
            return jnp.take(jnp.concatenate(pooled, axis=0), pick_index, axis=0)

        group_score = lax.all_gather(score, 'beam', tiled=True)
        parent_score = jnp.take(group_score, my_parent)
        residual = x_embed.astype(jnp.float32)
        k_layers = []
        v_layers = []
        for layer_idx in range(layers):
            k_sel = reorder(k_cache[layer_idx])
            v_sel = reorder(v_cache[layer_idx])
            residual, k_sel, v_sel = layer_body(residual, k_sel, v_sel, position, gain_attn[layer_idx], w_query[layer_idx], w_key[layer_idx], w_value[layer_idx], w_out[layer_idx], gain_mlp[layer_idx], w_gate[layer_idx], w_up[layer_idx], w_down[layer_idx])
            k_layers.append(k_sel)
            v_layers.append(v_sel)
        logits = jnp.dot(rms_norm(residual, gain_final), w_vocab, preferred_element_type=jnp.float32)
        candidates = parent_score[:, None] + vocab_log_softmax(logits)
        return jnp.stack(k_layers), jnp.stack(v_layers), candidates

    return jax.shard_map(local_step, mesh=mesh, in_specs=in_specs, out_specs=out_specs, check_vma=False)
```

profile of v0, /device:TPU:0, one launch (start us, length us, event | category | flops | bytes accessed | tf_op | source)
XLA Modules:
  0.0 598.3 jit_solution(1383771491428659289)
XLA Ops:
  8.1 5.6 slice_bitcast_fusion.4
  13.7 4.4 gather_fusion.1
  18.1 2.1 gather_fusion.3
  20.2 5.6 slice_bitcast_fusion
  25.8 3.6 gather_fusion.5
  29.4 3.6 gather_fusion.7
  33.0 3.6 gather_fusion.9
  36.6 3.6 gather_fusion.11
  40.2 3.6 gather_fusion.13
  45.8 12.3 %broadcast_select_fusion.8 = (bf16[16,256,4,64]{1,3,2,0:T(8,128)(2,1)}, bf16[16,256,4,64]{1,3,2,0:T(8,128)(2,1)}, bf16[16,256,4,64]{1,3,2,0:T(8,128)(2,1)}, bf16...) fusion(bf16[16,256,4,64]{1,3,2,0:T(8,128)(2,1)} %gather_fusion., ...), kind=kLoop, calls=%fused_computation.87 | loop fusion | flops 8388608 | bytes 33554448 | tf_op jit(solution)/shard_map/jit(_take)/select_n | solution.py:90
  61.2 2.9 slice_bitcast_fusion.11
  70.1 3.2 broadcast_in_dim_reshape.16
  73.3 4.6 pad_maximum_fusion.2
  77.9 4.2 gather_fusion.2
  82.1 4.6 pad_maximum_fusion.4
  86.7 4.3 gather_fusion.6
  91.0 4.6 pad_maximum_fusion.5
  95.6 4.2 gather_fusion.8
  99.8 4.6 pad_maximum_fusion.6
  104.4 4.2 gather_fusion.10
  108.5 4.6 pad_maximum_fusion.7
  113.1 4.2 gather_fusion.12
  117.3 4.6 pad_maximum_fusion.8
  121.9 4.2 gather_fusion.14
  126.1 4.6 pad_maximum_fusion.3
  130.7 4.3 gather_fusion.4
  135.0 4.0 pad_maximum_fusion.9
  138.9 4.3 gather_fusion.16
  143.3 10.6 %broadcast_select_fusion = (bf16[16,256,4,64]{1,3,2,0:T(8,128)(2,1)}, bf16[16,256,4,64]{1,3,2,0:T(8,128)(2,1)}, bf16[16,256,4,64]{1,3,2,0:T(8,128)(2,1)}, bf16[1...) fusion(bf16[16,256,4,64]{1,3,2,0:T(8,128)(2,1)} %gather_fusion., ...), kind=kLoop, calls=%fused_computation.79 | loop fusion | flops 8388608 | bytes 33554448 | tf_op jit(solution)/shard_map/jit(_take)/select_n | solution.py:92
  153.9 9.0 %dynamic_update_slice.24 = bf16[16,256,4,64]{1,3,2,0:T(8,128)(2,1)} dynamic-update-slice(bf16[16,256,4,64]{1,3,2,0:T(8,128)(2,1)} %get-tuple-element.78, bf16[16,1,4,64]{1,3,2,0:T(8,128)(2,1)S(1)} %copy.53, s32[]{:T(128)} %constant.112.clone.1, s32[]{:T(128)S(6)} %select_n.92, s32[]{:T(128)} %constant.112.clone.1, s32[]{:T(128)} %constant.112.clone.1) | dynamic-update-slice | bytes 16388 | tf_op jit(solution)/shard_map/dynamic_update_slice | solution.py:34
  162.9 2.1 fusion.182
  165.1 7.5 %dynamic_update_slice.25 = bf16[16,256,4,64]{1,3,2,0:T(8,128)(2,1)S(1)} dynamic-update-slice(bf16[16,256,4,64]{1,3,2,0:T(8,128)(2,1)S(1)} %copy-done.7, bf16[16,1,4,64]{1,3,2,0:T(8,128)(2,1)S(1)} %copy-done.9, s32[]{:T(128)} %constant.112.clone.1, s32[]{:T(128)S(6)} %select_n.92, s32[]{:T(128)} %constant.112.clone.1, s32[]{:T(128)} %constant.112.clone.1) | dynamic-update-slice | bytes 16388 | tf_op jit(solution)/shard_map/dynamic_update_slice | solution.py:35
  175.4 36.8 %all-reduce.10.cloned.1.call-done = f32[16,1024]{1,0:T(8,128)} async-done(((f32[16,1024]{1,0:T(8,128)}), f32[16,1024]{1,0:T(8,128)}) %all-reduce.10.cloned.1.call-update) | async-done | bytes 65552 | tf_op jit(solution)/shard_map/psum | solution.py:43
  216.1 3.6 fusion.26
  221.4 32.5 %all-reduce.12.cloned.1.call-done = f32[16,1024]{1,0:T(8,128)} async-done(((f32[16,1024]{1,0:T(8,128)}), f32[16,1024]{1,0:T(8,128)}) %all-reduce.12.cloned.1.call-update) | async-done | bytes 65552 | tf_op jit(solution)/shard_map/psum | solution.py:48
  257.7 7.5 %dynamic_update_slice.26 = bf16[16,256,4,64]{1,3,2,0:T(8,128)(2,1)S(1)} dynamic-update-slice(bf16[16,256,4,64]{1,3,2,0:T(8,128)(2,1)S(1)} %copy-done.5, bf16[16,1,4,64]{1,3,2,0:T(8,128)(2,1)S(1)} %copy.57, s32[]{:T(128)} %constant.112.clone.1, s32[]{:T(128)S(6)} %select_n.92, s32[]{:T(128)} %constant.112.clone.1, s32[]{:T(128)} %constant.112.clone.1) | dynamic-update-slice | bytes 16388 | tf_op jit(solution)/shard_map/dynamic_update_slice | solution.py:34
  265.8 2.1 broadcast_in_dim_reshape.17
  268.0 8.7 %dynamic_update_slice.27 = bf16[16,256,4,64]{1,3,2,0:T(8,128)(2,1)} dynamic-update-slice(bf16[16,256,4,64]{1,3,2,0:T(8,128)(2,1)} %get-tuple-element.75, bf16[16,1,4,64]{1,3,2,0:T(8,128)(2,1)S(1)} %broadcast_in_dim_reshape.17, s32[]{:T(128)} %constant.112.clone.1, s32[]{:T(128)S(6)} %select_n.92, s32[]{:T(128)} %constant.112.clone.1, s32[]{:T(128)} %constant.112.clone.1) | dynamic-update-slice | bytes 16388 | tf_op jit(solution)/shard_map/dynamic_update_slice | solution.py:35
  276.7 2.3 fusion.127
  283.0 5.6 all-reduce
  288.7 26.6 %all-reduce.14.cloned.1.call-done = f32[16,1024]{1,0:T(8,128)} async-done(((f32[16,1024]{1,0:T(8,128)}), f32[16,1024]{1,0:T(8,128)}) %all-reduce.14.cloned.1.call-update) | async-done | bytes 65552 | tf_op jit(solution)/shard_map/psum | solution.py:43
  316.2 2.0 fusion.24
  318.2 3.6 fusion.20
  321.9 34.1 %all-reduce.16.cloned.1.call-done = f32[16,1024]{1,0:T(8,128)} async-done(((f32[16,1024]{1,0:T(8,128)}), f32[16,1024]{1,0:T(8,128)}) %all-reduce.16.cloned.1.call-update) | async-done | bytes 65552 | tf_op jit(solution)/shard_map/psum | solution.py:48
  359.8 7.8 %dynamic_update_slice.28 = bf16[16,256,4,64]{1,3,2,0:T(8,128)(2,1)S(1)} dynamic-update-slice(bf16[16,256,4,64]{1,3,2,0:T(8,128)(2,1)S(1)} %copy-done.3, bf16[16,1,4,64]{1,3,2,0:T(8,128)(2,1)S(1)} %copy.61, s32[]{:T(128)} %constant.112.clone.1, s32[]{:T(128)S(6)} %select_n.92, s32[]{:T(128)} %constant.112.clone.1, s32[]{:T(128)} %constant.112.clone.1) | dynamic-update-slice | bytes 16388 | tf_op jit(solution)/shard_map/dynamic_update_slice | solution.py:34
  368.2 2.1 broadcast_in_dim_reshape.18
  370.3 8.7 %dynamic_update_slice.29 = bf16[16,256,4,64]{1,3,2,0:T(8,128)(2,1)} dynamic-update-slice(bf16[16,256,4,64]{1,3,2,0:T(8,128)(2,1)} %get-tuple-element.77, bf16[16,1,4,64]{1,3,2,0:T(8,128)(2,1)S(1)} %broadcast_in_dim_reshape.18, s32[]{:T(128)} %constant.112.clone.1, s32[]{:T(128)S(6)} %select_n.92, s32[]{:T(128)} %constant.112.clone.1, s32[]{:T(128)} %constant.112.clone.1) | dynamic-update-slice | bytes 16388 | tf_op jit(solution)/shard_map/dynamic_update_slice | solution.py:35
  379.0 2.2 fusion.125
  384.0 33.5 %all-reduce.18.cloned.1.call-done = f32[16,1024]{1,0:T(8,128)} async-done(((f32[16,1024]{1,0:T(8,128)}), f32[16,1024]{1,0:T(8,128)}) %all-reduce.18.cloned.1.call-update) | async-done | bytes 65552 | tf_op jit(solution)/shard_map/psum | solution.py:43
  420.4 3.6 fusion.14
  425.9 32.4 %all-reduce.20.cloned.1.call-done = f32[16,1024]{1,0:T(8,128)} async-done(((f32[16,1024]{1,0:T(8,128)}), f32[16,1024]{1,0:T(8,128)}) %all-reduce.20.cloned.1.call-update) | async-done | bytes 65552 | tf_op jit(solution)/shard_map/psum | solution.py:48
  462.0 7.5 %dynamic_update_slice.30 = bf16[16,256,4,64]{1,3,2,0:T(8,128)(2,1)S(1)} dynamic-update-slice(bf16[16,256,4,64]{1,3,2,0:T(8,128)(2,1)S(1)} %copy-done.2, bf16[16,1,4,64]{1,3,2,0:T(8,128)(2,1)S(1)} %copy.65, s32[]{:T(128)} %constant.112.clone.1, s32[]{:T(128)S(6)} %select_n.92, s32[]{:T(128)} %constant.112.clone.1, s32[]{:T(128)} %constant.112.clone.1) | dynamic-update-slice | bytes 16388 | tf_op jit(solution)/shard_map/dynamic_update_slice | solution.py:34
  470.2 2.1 broadcast_in_dim_reshape.19
  472.3 8.7 %dynamic_update_slice.31 = bf16[16,256,4,64]{1,3,2,0:T(8,128)(2,1)} dynamic-update-slice(bf16[16,256,4,64]{1,3,2,0:T(8,128)(2,1)} %get-tuple-element.71, bf16[16,1,4,64]{1,3,2,0:T(8,128)(2,1)S(1)} %broadcast_in_dim_reshape.19, s32[]{:T(128)} %constant.112.clone.1, s32[]{:T(128)S(6)} %select_n.92, s32[]{:T(128)} %constant.112.clone.1, s32[]{:T(128)} %constant.112.clone.1) | dynamic-update-slice | bytes 16388 | tf_op jit(solution)/shard_map/dynamic_update_slice | solution.py:35
  481.0 2.2 fusion.123
  485.2 7.4 %pad_maximum_fusion.1 = bf16[4,16,256,4,64]{2,4,3,1,0:T(8,128)(2,1)} fusion(bf16[1,16,256,4,64]{2,4,3,1,0:T(8,128)(2,1)} %bitcast.286, bf16[1,16,256,4,64]{2,4,3,1,0:T(8,128)(2,1)} %bitcast.287, bf16[1,16,256,4,64]{2,4,3,1,0:T(8,128)(2,1)} %bitcast.288, bf16[1,16,256,4,64]{2,4,3,1,0:T(8,128)(2,1)} %bitcast.289), kind=kLoop, calls=%fused_computation.26 | loop fusion | flops 12582912 | bytes 16777216 | tf_op jit(solution)/shard_map/stack | solution.py:107
  492.7 26.7 %all-reduce.22.cloned.1.call-done = f32[16,1024]{1,0:T(8,128)} async-done(((f32[16,1024]{1,0:T(8,128)}), f32[16,1024]{1,0:T(8,128)}) %all-reduce.22.cloned.1.call-update) | async-done | bytes 65552 | tf_op jit(solution)/shard_map/psum | solution.py:43
  520.4 2.0 fusion.12
  522.4 3.6 fusion.8
  526.0 6.6 %pad_maximum_fusion = bf16[4,16,256,4,64]{2,4,3,1,0:T(8,128)(2,1)} fusion(bf16[1,16,256,4,64]{2,4,3,1,0:T(8,128)(2,1)S(1)} %bitcast.282, bf16[1,16,256,4,64]{2,4,3,1,0:T(8,128)(2,1)} %bitcast.283, bf16[1,16,256,4,64]{2,4,3,1,0:T(8,128)(2,1)} %bitcast.284, bf16[1,16,256,4,64]{2,4,3,1,0:T(8,128)(2,1)} %bitcast.285), kind=kLoop, calls=%fused_computation.25 | loop fusion | flops 12582912 | bytes 16777216 | tf_op jit(solution)/shard_map/stack | solution.py:107
  532.6 27.6 %all-reduce.24.cloned.1.call-done = f32[16,1024]{1,0:T(8,128)} async-done(((f32[16,1024]{1,0:T(8,128)}), f32[16,1024]{1,0:T(8,128)}) %all-reduce.24.cloned.1.call-update) | async-done | bytes 65552 | tf_op jit(solution)/shard_map/psum | solution.py:48
  561.2 10.2 %fusion.230 = (f32[16]{0:T(128)S(1)}, f32[16,8032]{1,0:T(8,128)S(1)}) fusion(bf16[1024,8032]{0,1:T(8,128)(2,1)} %param.37, f32[16,1024]{1,0:T(8,128)S(1)} %get-tuple-element.6, f32[1024]{0:T(1024)S(1)} %convert_element_type.185, f32[16]{0:T(128)S(1)} %add_rsqrt_fusion), kind=kOutput, calls=%fused_computation.348 | convolution fusion | flops 263370224 | bytes 17033344 | tf_op jit(solution)/shard_map/dot_general | solution.py:105
  571.4 10.5 %pmax.7 = f32[16]{0:T(128)S(1)} all-reduce(f32[16]{0:T(128)S(1)} %get-tuple-element.89), channel_id=1, replica_groups=mesh['data'=2,'model'=4,'beam'=4] {'model'}, use_global_device_ids=true, to_apply=%region_26.29 | all-reduce | flops 16 | bytes 128 | tf_op jit(solution)/shard_map/pmax | solution.py:54
  582.2 8.4 %psum.71 = f32[16,1]{0,1:T(1,128)S(1)} all-reduce(f32[16,1]{0,1:T(1,128)S(1)} %bitcast.315), channel_id=1, replica_groups=mesh['data'=2,'model'=4,'beam'=4] {'model'}, use_global_device_ids=true, to_apply=%region_28.31 | all-reduce | flops 16 | bytes 128 | tf_op jit(solution)/shard_map/psum | solution.py:55
  (177 shorter events, 49.7 us)
Async XLA Ops:
  7.2 205.1 %all-reduce.10.cloned.1.call-start = ((), (), s32[]{:S(2)}) async-start(), calls=%async_computation | async-start | bytes 131072 | tf_op jit(solution)/shard_map/psum | solution.py:43
  13.7 4.4 copy-start
  45.8 13.9 %copy-start.10 = (bf16[4,1024,256]{2,1,0:T(8,128)(2,1)S(1)}, bf16[4,1024,256]{2,1,0:T(8,128)(2,1)}, u32[]{:S(2)}) copy-start(bf16[4,1024,256]{2,1,0:T(8,128)(2,1)} %param.28) | copy-start | bytes 6291460
  58.1 8.7 %collective-permute-start = (bf16[16,256,4,64]{1,3,2,0:T(8,128)(2,1)}, bf16[16,256,4,64]{1,3,2,0:T(8,128)(2,1)}, u32[]{:S(2)}, u32[]{:S(2)}) collective-permute-start(bf16[16,256,4,64]{1,3,2,0:T(8,128)(2,1)} %get-tuple-element.86), channel_id=1, source_target_pairs={{0,1},{1,0},{2,3},{3,2},{4,5},{5,4},{6,7},{7,6},{8,9},{9,8},{10,11... | collective-permute-start | bytes 6291464 | tf_op jit(solution)/shard_map/ppermute | solution.py:91
  58.7 8.2 %collective-permute-start.2 = (bf16[16,256,4,64]{1,3,2,0:T(8,128)(2,1)}, bf16[16,256,4,64]{1,3,2,0:T(8,128)(2,1)}, u32[]{:S(2)}, u32[]{:S(2)}) collective-permute-start(bf16[16,256,4,64]{1,3,2,0:T(8,128)(2,1)} %get-tuple-element.81), channel_id=1, source_target_pairs={{0,1},{1,0},{2,3},{3,2},{4,5},{5,4},{6,7},{7,6},{8,9},{9,8},{10,11... | collective-permute-start | bytes 6291464 | tf_op jit(solution)/shard_map/ppermute | solution.py:91
  58.8 9.7 %collective-permute-start.3 = (bf16[16,256,4,64]{1,3,2,0:T(8,128)(2,1)}, bf16[16,256,4,64]{1,3,2,0:T(8,128)(2,1)}, u32[]{:S(2)}, u32[]{:S(2)}) collective-permute-start(bf16[16,256,4,64]{1,3,2,0:T(8,128)(2,1)} %get-tuple-element.82), channel_id=1, source_target_pairs={{0,1},{1,0},{2,3},{3,2},{4,5},{5,4},{6,7},{7,6},{8,9},{9,8},{10,11... | collective-permute-start | bytes 6291464 | tf_op jit(solution)/shard_map/ppermute | solution.py:91
  59.2 40.6 %collective-permute-start.4 = (bf16[16,256,4,64]{1,3,2,0:T(8,128)(2,1)}, bf16[16,256,4,64]{1,3,2,0:T(8,128)(2,1)}, u32[]{:S(2)}, u32[]{:S(2)}) collective-permute-start(bf16[16,256,4,64]{1,3,2,0:T(8,128)(2,1)} %get-tuple-element.83), channel_id=1, source_target_pairs={{0,1},{1,0},{2,3},{3,2},{4,5},{5,4},{6,7},{7,6},{8,9},{9,8},{10,11... | collective-permute-start | bytes 6291464 | tf_op jit(solution)/shard_map/ppermute | solution.py:91
  59.3 49.2 %collective-permute-start.5 = (bf16[16,256,4,64]{1,3,2,0:T(8,128)(2,1)}, bf16[16,256,4,64]{1,3,2,0:T(8,128)(2,1)}, u32[]{:S(2)}, u32[]{:S(2)}) collective-permute-start(bf16[16,256,4,64]{1,3,2,0:T(8,128)(2,1)} %get-tuple-element.84), channel_id=1, source_target_pairs={{0,1},{1,0},{2,3},{3,2},{4,5},{5,4},{6,7},{7,6},{8,9},{9,8},{10,11... | collective-permute-start | bytes 6291464 | tf_op jit(solution)/shard_map/ppermute | solution.py:91
  61.1 4.8 copy-start.15
  61.1 5.0 copy-start.17
  66.8 50.5 %collective-permute-start.6 = (bf16[16,256,4,64]{1,3,2,0:T(8,128)(2,1)}, bf16[16,256,4,64]{1,3,2,0:T(8,128)(2,1)}, u32[]{:S(2)}, u32[]{:S(2)}) collective-permute-start(bf16[16,256,4,64]{1,3,2,0:T(8,128)(2,1)} %get-tuple-element.85), channel_id=1, source_target_pairs={{0,1},{1,0},{2,3},{3,2},{4,5},{5,4},{6,7},{7,6},{8,9},{9,8},{10,11... | collective-permute-start | bytes 6291464 | tf_op jit(solution)/shard_map/ppermute | solution.py:91
  67.0 59.2 %collective-permute-start.1 = (bf16[16,256,4,64]{1,3,2,0:T(8,128)(2,1)}, bf16[16,256,4,64]{1,3,2,0:T(8,128)(2,1)}, u32[]{:S(2)}, u32[]{:S(2)}) collective-permute-start(bf16[16,256,4,64]{1,3,2,0:T(8,128)(2,1)} %get-tuple-element.80), channel_id=1, source_target_pairs={{0,1},{1,0},{2,3},{3,2},{4,5},{5,4},{6,7},{7,6},{8,9},{9,8},{10,11... | collective-permute-start | bytes 6291464 | tf_op jit(solution)/shard_map/ppermute | solution.py:91
  68.5 66.5 %collective-permute-start.7 = (bf16[16,256,4,64]{1,3,2,0:T(8,128)(2,1)}, bf16[16,256,4,64]{1,3,2,0:T(8,128)(2,1)}, u32[]{:S(2)}, u32[]{:S(2)}) collective-permute-start(bf16[16,256,4,64]{1,3,2,0:T(8,128)(2,1)} %get-tuple-element.79), channel_id=1, source_target_pairs={{0,1},{1,0},{2,3},{3,2},{4,5},{5,4},{6,7},{7,6},{8,9},{9,8},{10,11... | collective-permute-start | bytes 6291464 | tf_op jit(solution)/shard_map/ppermute | solution.py:91
  138.9 4.3 copy-start.1
  153.9 11.2 %copy-start.7 = (bf16[16,256,4,64]{1,3,2,0:T(8,128)(2,1)S(1)}, bf16[16,256,4,64]{1,3,2,0:T(8,128)(2,1)}, u32[]{:S(2)}) copy-start(bf16[16,256,4,64]{1,3,2,0:T(8,128)(2,1)} %get-tuple-element.73) | copy-start | bytes 6291460
  162.9 2.3 copy-start.9
  165.1 10.3 %copy-start.18 = (bf16[4,1024]{1,0:T(4,128)(2,1)S(1)}, bf16[4,1024]{1,0:T(4,128)(2,1)}, u32[]{:S(2)}) copy-start(bf16[4,1024]{1,0:T(4,128)(2,1)} %param.32) | copy-start | bytes 24580
  172.7 43.4 %copy-start.8 = (bf16[16,256,4,64]{1,3,2,0:T(8,128)(2,1)}, bf16[16,256,4,64]{1,3,2,0:T(8,128)(2,1)S(1)}, u32[]{:S(2)}) copy-start(bf16[16,256,4,64]{1,3,2,0:T(8,128)(2,1)S(1)} %dynamic_update_slice.25) | copy-start | bytes 6291460
  175.3 78.6 %all-reduce.12.cloned.1.call-start = ((), (), s32[]{:S(2)}) async-start(), calls=%async_computation.1 | async-start | bytes 131072 | tf_op jit(solution)/shard_map/psum | solution.py:48
  216.1 3.7 copy-start.14
  219.7 34.2 %copy-start.16 = (f32[16,1024]{1,0:T(8,128)S(1)}, f32[16,1024]{1,0:T(8,128)}, u32[]{:S(2)}) copy-start(f32[16,1024]{1,0:T(8,128)} %all-reduce.10.cloned.1.call-done) | copy-start | bytes 196612
  219.7 95.5 %all-reduce.14.cloned.1.call-start = ((), (), s32[]{:S(2)}) async-start(), calls=%async_computation.2 | async-start | bytes 131072 | tf_op jit(solution)/shard_map/psum | solution.py:43
  220.0 37.7 %copy-start.5 = (bf16[16,256,4,64]{1,3,2,0:T(8,128)(2,1)S(1)}, bf16[16,256,4,64]{1,3,2,0:T(8,128)(2,1)}, u32[]{:S(2)}) copy-start(bf16[16,256,4,64]{1,3,2,0:T(8,128)(2,1)} %get-tuple-element.72) | copy-start | bytes 6291460
  265.2 11.4 %copy-start.6 = (bf16[16,256,4,64]{1,3,2,0:T(8,128)(2,1)}, bf16[16,256,4,64]{1,3,2,0:T(8,128)(2,1)S(1)}, u32[]{:S(2)}) copy-start(bf16[16,256,4,64]{1,3,2,0:T(8,128)(2,1)S(1)} %dynamic_update_slice.26) | copy-start | bytes 6291460
  276.7 4.4 copy-start.12
  276.7 4.9 copy-start.21
  276.7 6.1 %copy-start.20 = (f32[16]{0:T(128)S(1)}, f32[16]{0:T(128)}, u32[]{:S(2)}) copy-start(f32[16]{0:T(128)} %param.24) | copy-start | bytes 196
  279.0 2.3 copy-start.13
  281.0 75.0 %all-reduce.16.cloned.1.call-start = ((), (), s32[]{:S(2)}) async-start(), calls=%async_computation.3 | async-start | bytes 131072 | tf_op jit(solution)/shard_map/psum | solution.py:48
  321.8 38.0 %copy-start.3 = (bf16[16,256,4,64]{1,3,2,0:T(8,128)(2,1)S(1)}, bf16[16,256,4,64]{1,3,2,0:T(8,128)(2,1)}, u32[]{:S(2)}) copy-start(bf16[16,256,4,64]{1,3,2,0:T(8,128)(2,1)} %get-tuple-element.74) | copy-start | bytes 6291460
  321.8 95.6 %all-reduce.18.cloned.1.call-start = ((), (), s32[]{:S(2)}) async-start(), calls=%async_computation.4 | async-start | bytes 131072 | tf_op jit(solution)/shard_map/psum | solution.py:43
  367.6 11.4 %copy-start.4 = (bf16[16,256,4,64]{1,3,2,0:T(8,128)(2,1)}, bf16[16,256,4,64]{1,3,2,0:T(8,128)(2,1)S(1)}, u32[]{:S(2)}) copy-start(bf16[16,256,4,64]{1,3,2,0:T(8,128)(2,1)S(1)} %dynamic_update_slice.28) | copy-start | bytes 6291460
  383.2 75.1 %all-reduce.20.cloned.1.call-start = ((), (), s32[]{:S(2)}) async-start(), calls=%async_computation.5 | async-start | bytes 131072 | tf_op jit(solution)/shard_map/psum | solution.py:48
  420.4 3.8 copy-start.11
  424.1 1.8 copy-start.19
  424.1 95.3 %all-reduce.22.cloned.1.call-start = ((), (), s32[]{:S(2)}) async-start(), calls=%async_computation.6 | async-start | bytes 131072 | tf_op jit(solution)/shard_map/psum | solution.py:43
  424.4 37.6 %copy-start.2 = (bf16[16,256,4,64]{1,3,2,0:T(8,128)(2,1)S(1)}, bf16[16,256,4,64]{1,3,2,0:T(8,128)(2,1)}, u32[]{:S(2)}) copy-start(bf16[16,256,4,64]{1,3,2,0:T(8,128)(2,1)} %get-tuple-element.76) | copy-start | bytes 6291460
  485.2 75.0 %all-reduce.24.cloned.1.call-start = ((), (), s32[]{:S(2)}) async-start(), calls=%async_computation.7 | async-start | bytes 131072 | tf_op jit(solution)/shard_map/psum | solution.py:48
Sparse Core Ops, SparseCore 0:
  175.5 36.7 all-reduce.9
  219.9 34.0 all-reduce.11
  281.1 34.0 all-reduce.13
  321.9 34.0 all-reduce.15
  383.3 34.0 all-reduce.17
  424.2 34.0 all-reduce.19
  485.3 34.0 all-reduce.21
  526.1 34.0 all-reduce.23
where the time goes:
time: 601 us; the launch traced here: 598 us
  waiting for transfers between devices  251 us (42%)
  local copies, waits for them, and re-layouts  160 us (27%)
  other arithmetic  85.6 us (14%)
  matrix products  58.2 us (10%)
  blocking collectives  24.5 us (4%)
  between operations  16 us (3%)
    psum x4, waiting for transfers between devices, layer_body(): lax.psum(jnp.dot(hidden, w_down, preferred_element_type=jnp.float32), 'mo...  127 us
    psum x4, waiting for transfers between devices, layer_body(): residual = residual + lax.psum(attn_part, 'model')  124 us
    concatenate x8, other arithmetic, reorder(): return jnp.take(jnp.concatenate(pooled, axis=0), pick_index, axis=0)  36.1 us
    gather x8, local copies, waits for them, and re-layouts, reorder(): return jnp.take(jnp.concatenate(pooled, axis=0), pick_index, axis=0)  33.8 us
    dynamic_update_slice x4, local copies, waits for them, and re-layouts, layer_body(): v_sel = lax.dynamic_update_slice(v_sel, v_new[:, None], (0, position, 0, 0))  33.6 us
    dynamic_update_slice x4, local copies, waits for them, and re-layouts, layer_body(): k_sel = lax.dynamic_update_slice(k_sel, k_new[:, None], (0, position, 0, 0))  31.8 us
    gather x8, local copies, waits for them, and re-layouts, reorder(): outgoing = jnp.take(cache_layer, send_index[step_idx], axis=0)  26.4 us
    dot_general x4, matrix products, layer_body(): jnp.dot(hidden, w_down, preferred_element_type=jnp.float32)  14.4 us
  transfers between devices with their start and end apart: 16, of which 9 were waited for; matrix products, arithmetic and copies ran while one was open for 15% of the time, Pallas kernels for 0%

commit v1 on v0

v1 whole, which is shorter than its diff:
```python
import functools

import jax
import jax.numpy as jnp
from jax import lax
from jax.experimental import pallas as pl
from jax.experimental.pallas import tpu as pltpu
from jax.sharding import PartitionSpec as P

NORM_EPS = 1e-6
ROPE_BASE = 10000.0
MESH = pl.DeviceIdType.MESH
F32 = jnp.float32
BF16 = jnp.bfloat16


def rms(res, gain):
    inv = lax.rsqrt(jnp.mean(res * res, axis=-1, keepdims=True) + NORM_EPS)
    return (res * inv * gain.astype(F32)).astype(BF16)


def dot(a, b):
    return jnp.dot(a, b, preferred_element_type=F32)


def dot_t(a, b):
    return lax.dot_general(a, b, (((1,), (1,)), ((), ())), preferred_element_type=F32)


def decode_kernel(cfg, *refs):
    L, B, D, HD, S, KH, FF, V, NM, SPAN = cfg
    (rows_ref, pos_ref, x_ref, rowsv_ref, score_ref, cos_ref, sin_ref, ga_ref, gm_ref, gf_ref,
     kc, vc, wq, wk, wv, wo, wg, wu, wd, wt, ko, vo, cand_ref) = refs[:23]
    scratch = list(refs[23:])
    kb = scratch[:L]
    vb = scratch[L:2 * L]
    (wqb, wkb, wvb, wob, wgb, wub, wdb, kst, vst, ar, stat, scb, res, qs, lg, pr, osc, lgt,
     sem_c, sem_w, sem_t, sem_st, bsend, brecv, asend, arecv, ssend, srecv, csend, crecv) = scratch[2 * L:]
    C = KH * HD
    me = lax.axis_index("model")
    beam = lax.axis_index("beam")
    spos = lax.rem(beam, SPAN)
    partner = beam - spos + lax.rem(spos + 1, SPAN)
    own = pl.ds(spos * B, B)

    def cache_local(l):
        return (pltpu.make_async_copy(kc.at[l], kb[l].at[own], sem_c.at[2 * l]),
                pltpu.make_async_copy(vc.at[l], vb[l].at[own], sem_c.at[2 * l + 1]))

    def cache_push(l):
        return tuple(pltpu.make_async_remote_copy(src_ref=c.at[l], dst_ref=buf[l].at[own], send_sem=bsend.at[2 * l + i],
                                                  recv_sem=brecv.at[2 * l + i], device_id={"beam": partner}, device_id_type=MESH)
                     for i, (c, buf) in enumerate(((kc, kb), (vc, vb))))

    weights = ((wq, wqb), (wk, wkb), (wv, wvb), (wo, wob), (wg, wgb), (wu, wub), (wd, wdb))

    def weight(l, i):
        src, buf = weights[i]
        return pltpu.make_async_copy(src.at[l], buf.at[l % 2], sem_w.at[(l % 2) * 7 + i])

    chunks = (kb[0], vb[0], kb[1], vb[1])
    CW = S
    NCH = D // CW

    NT = lgt.shape[0]
    TN = lgt.shape[2]

    def vocab(c, n, rows=TN):
        start = n * TN if isinstance(n, int) else pl.multiple_of(n * TN, TN)
        return pltpu.make_async_copy(wt.at[pl.ds(start, rows), c * CW:(c + 1) * CW], chunks[c].at[n, pl.ds(0, rows)],
                                     sem_t.at[c * NT + n])

    def vocab_all(act):
        def body(n, carry):
            for c in range(NCH):
                act(vocab(c, n))
            return carry
        full = V // TN
        lax.fori_loop(0, full, body, 0)
        if full < NT:
            for c in range(NCH):
                act(vocab(c, full, V - full * TN))

    for i in range(3):
        weight(0, i).start()
    for c in cache_local(0):
        c.start()

    barrier = pltpu.get_barrier_semaphore()
    for k in range(1, NM):
        pl.semaphore_signal(barrier, inc=1, device_id={"model": lax.rem(me + k, NM)}, device_id_type=MESH)
    pl.semaphore_signal(barrier, inc=1, device_id={"beam": partner}, device_id_type=MESH)
    pl.semaphore_wait(barrier, NM)

    for c in cache_push(0):
        c.start()
    score_copy = pltpu.make_async_remote_copy(src_ref=score_ref, dst_ref=scb.at[0], send_sem=csend, recv_sem=crecv,
                                              device_id={"beam": partner}, device_id_type=MESH)
    score_copy.start()
    for i in range(3, 7):
        weight(0, i).start()
    for i in range(7):
        weight(1, i).start()

    def reduce_copies(step):
        slot = step * NM + me
        return [pltpu.make_async_remote_copy(src_ref=ar.at[slot], dst_ref=ar.at[slot], send_sem=asend.at[step * (NM - 1) + k - 1],
                                             recv_sem=arecv.at[step * (NM - 1) + k - 1],
                                             device_id={"model": lax.rem(me + k, NM)}, device_id_type=MESH)
                for k in range(1, NM)]

    def reduce_start(step, value):
        ar[step * NM + me] = value
        copies = reduce_copies(step)
        for c in copies:
            c.start()
        return copies

    def reduce_finish(step, copies):
        for c in copies:
            c.wait_recv()
        total = ar[step * NM]
        for k in range(1, NM):
            total = total + ar[step * NM + k]
        return total

    pos = pos_ref[0]
    cos = cos_ref[...]
    sin = sin_ref[...]
    low = lax.rem(lax.broadcasted_iota(jnp.int32, (B, C), 1), HD) < HD // 2

    def rope(x):
        other = jnp.where(low, -pltpu.roll(x, C - HD // 2, 1), pltpu.roll(x, HD // 2, 1))
        return x * cos + other * sin

    head_of_lane = lax.broadcasted_iota(jnp.int32, (8, C), 1) // HD
    head_mask = head_of_lane == lax.broadcasted_iota(jnp.int32, (8, C), 0)
    slot = lax.broadcasted_iota(jnp.int32, (C, S), 1)
    here = slot == pos
    res[...] = x_ref[...].astype(F32)
    sends = [score_copy]

    for l in range(L):
        ws = l % 2
        h = rms(res[...], ga_ref[l:l + 1, :])
        for i in range(3):
            weight(l, i).wait()
        q = rope(dot(h, wqb[ws])).astype(BF16).astype(F32)
        k = rope(dot(h, wkb[ws])).astype(BF16).astype(F32)
        v = dot(h, wvb[ws]).astype(BF16).astype(F32)
        qs[...] = q * (HD ** -0.5)
        pad = jnp.zeros((128 - B, C), F32)
        k_cols = jnp.concatenate([k, pad], axis=0).T
        v_cols = jnp.concatenate([v, pad], axis=0).T
        for c in cache_local(l):
            c.wait()
        pushes = cache_push(l)
        pushes[0].wait_recv()
        if l > 0:
            pltpu.make_async_copy(kst, ko.at[l - 1], sem_st.at[0]).wait()
        for b in range(B):
            kept = jnp.where(here, jnp.broadcast_to(k_cols[:, b:b + 1], (C, S)).astype(BF16), kb[l][rows_ref[b]])
            kst[b] = kept
            qb = jnp.where(head_mask, jnp.broadcast_to(qs[b:b + 1, :], (8, C)), 0.0).astype(BF16)
            lg[b * 8:(b + 1) * 8, :] = dot(qb, kept)
        pltpu.make_async_copy(kst, ko.at[l], sem_st.at[0]).start()
        logits = lg[...]
        logits = jnp.where(lax.broadcasted_iota(jnp.int32, logits.shape, 1) <= pos, logits, -jnp.inf)
        e = jnp.exp(logits - jnp.max(logits, axis=-1, keepdims=True))
        pr[...] = e / jnp.sum(e, axis=-1, keepdims=True)
        pushes[1].wait_recv()
        if l > 0:
            pltpu.make_async_copy(vst, vo.at[l - 1], sem_st.at[1]).wait()
        for b in range(B):
            kept = jnp.where(here, jnp.broadcast_to(v_cols[:, b:b + 1], (C, S)).astype(BF16), vb[l][rows_ref[b]])
            vst[b] = kept
            ob = dot_t(pr[b * 8:(b + 1) * 8, :].astype(BF16), kept)
            osc[b:b + 1, :] = jnp.sum(jnp.where(head_mask, ob, 0.0), axis=0, keepdims=True)
        pltpu.make_async_copy(vst, vo.at[l], sem_st.at[1]).start()
        weight(l, 3).wait()
        copies = reduce_start(2 * l, dot(osc[...].astype(BF16), wob[ws]))
        sends += copies
        if l + 1 < L:
            for c in cache_local(l + 1):
                c.start()
            for c in cache_push(l + 1):
                c.start()
            if l + 2 < L:
                for i in range(4):
                    weight(l + 2, i).start()
        sends += list(pushes)
        if l == 2:
            vocab_all(lambda c: c.start())
        r = res[...] + reduce_finish(2 * l, copies)
        h = rms(r, gm_ref[l:l + 1, :])
        weight(l, 4).wait()
        weight(l, 5).wait()
        gate = dot(h, wgb[ws])
        up = dot(h, wub[ws])
        g = (gate * jax.nn.sigmoid(gate) * up).astype(BF16)
        weight(l, 6).wait()
        copies = reduce_start(2 * l + 1, dot(g, wdb[ws]))
        sends += copies
        if l + 2 < L:
            for i in range(4, 7):
                weight(l + 2, i).start()
        res[...] = r + reduce_finish(2 * l + 1, copies)

    h = rms(res[...], gf_ref[...])
    vocab_all(lambda c: c.wait())

    def tile(n, carry):
        acc = dot_t(h[:, 0:CW], chunks[0][n])
        for c in range(1, NCH):
            acc = acc + dot_t(h[:, c * CW:(c + 1) * CW], chunks[c][n])
        acc = jnp.where(lax.broadcasted_iota(jnp.int32, (B, TN), 1) + n * TN < V, acc, -jnp.inf)
        lgt[n] = acc
        return jnp.maximum(carry, acc)

    peak = lax.fori_loop(0, NT, tile, jnp.full((B, TN), -jnp.inf, F32))
    m = jnp.max(peak, axis=-1, keepdims=True)

    def add_exp(n, carry):
        return carry + jnp.exp(lgt[n] - m)

    s = jnp.sum(lax.fori_loop(0, NT, add_exp, jnp.zeros((B, TN), F32)), axis=-1, keepdims=True)
    stat[me, 0] = jnp.broadcast_to(m, (B, 128))
    stat[me, 1] = jnp.broadcast_to(s, (B, 128))
    copies = [pltpu.make_async_remote_copy(src_ref=stat.at[me], dst_ref=stat.at[me], send_sem=ssend.at[k - 1], recv_sem=srecv.at[k - 1],
                                           device_id={"model": lax.rem(me + k, NM)}, device_id_type=MESH) for k in range(1, NM)]
    for c in copies:
        c.start()
    sends += copies
    score_copy.wait_recv()
    mine = score_ref[0:1, :]
    theirs = scb[0, 0:1, :]
    lane = lax.broadcasted_iota(jnp.int32, (B, 128), 1)
    want = rowsv_ref[...]
    first = jnp.where(spos == 0, mine, theirs)
    second = jnp.where(spos == 0, theirs, mine)
    parent_score = jnp.sum(jnp.where(lane == want, first, 0.0) + jnp.where(lane == want - B, second, 0.0), axis=-1, keepdims=True)
    for c in copies:
        c.wait_recv()
    gm = stat[0, 0]
    for k in range(1, NM):
        gm = jnp.maximum(gm, stat[k, 0])
    gs = stat[0, 1] * jnp.exp(stat[0, 0] - gm)
    for k in range(1, NM):
        gs = gs + stat[k, 1] * jnp.exp(stat[k, 0] - gm)
    gm = gm[:, 0:1]
    log_s = jnp.log(gs)[:, 0:1]
    for n in range(NT):
        hi = min((n + 1) * TN, V)
        cand_ref[:, n * TN:hi] = parent_score + ((lgt[n] - gm) - log_s)[:, :hi - n * TN]
    pltpu.make_async_copy(kst, ko.at[L - 1], sem_st.at[0]).wait()
    pltpu.make_async_copy(vst, vo.at[L - 1], sem_st.at[1]).wait()
    for c in sends:
        c.wait_send()


def solution(mesh):
    data_beam = ('data', 'beam')
    cache_spec = P(None, data_beam, None, 'model', None)
    col_spec = P(None, None, 'model')
    row_spec = P(None, 'model', None)
    in_specs = (P(data_beam, None), P('data', None), P(), P(data_beam), cache_spec, cache_spec,
                P(), col_spec, col_spec, col_spec, row_spec, P(), col_spec, col_spec, row_spec, P(), P(None, 'model'))
    out_specs = (cache_spec, cache_spec, P(data_beam, 'model'))
    n_model = mesh.shape['model']

    def local_step(x_embed, parent, position, score, k_cache, v_cache, gain_attn, w_query, w_key, w_value, w_out, gain_mlp,
                   w_gate, w_up, w_down, gain_final, w_vocab):
        L, B, S, KH, HD = k_cache.shape
        D = x_embed.shape[1]
        C = KH * HD
        FF = w_gate.shape[2]
        V = w_vocab.shape[1]
        span = parent.shape[1] // B
        my_index = lax.axis_index('beam')
        base = (my_index // span) * span * B
        rows = lax.dynamic_slice(parent.reshape(-1), (my_index * B,), (B,)) - base
        half = HD // 2
        inv_freq = ROPE_BASE ** (-jnp.arange(half, dtype=F32) / half)
        angles = position.astype(F32) * inv_freq
        cos = jnp.tile(jnp.cos(angles), 2 * KH)[None]
        sin = jnp.tile(jnp.sin(angles), 2 * KH)[None]
        flat = lambda c: jnp.transpose(c, (0, 1, 3, 4, 2)).reshape(L, B, C, S)
        score_pad = jnp.broadcast_to(jnp.pad(score, (0, 128 - B))[None], (8, 128))
        cfg = (L, B, D, HD, S, KH, FF, V, n_model, span)
        any_spec = pl.BlockSpec(memory_space=pl.ANY)
        vm = pl.BlockSpec(memory_space=pltpu.VMEM)
        sm = pl.BlockSpec(memory_space=pltpu.SMEM)
        steps = 2 * L
        TN = C
        NT = -(-V // TN)
        dma = pltpu.SemaphoreType.DMA
        scratch = ([pltpu.VMEM((span * B, C, S), BF16) for _ in range(2 * L)]
                   + [pltpu.VMEM((2, D, C), BF16)] * 3 + [pltpu.VMEM((2, C, D), BF16)]
                   + [pltpu.VMEM((2, D, FF), BF16)] * 2 + [pltpu.VMEM((2, FF, D), BF16)]
                   + [pltpu.VMEM((B, C, S), BF16)] * 2
                   + [pltpu.VMEM((steps * n_model, B, D), F32), pltpu.VMEM((n_model, 2, B, 128), F32), pltpu.VMEM((1, 8, 128), F32),
                      pltpu.VMEM((B, D), F32), pltpu.VMEM((B, C), F32), pltpu.VMEM((B * 8, S), F32), pltpu.VMEM((B * 8, S), F32),
                      pltpu.VMEM((B, C), F32), pltpu.VMEM((NT, B, TN), F32),
                      dma((2 * L,)), dma((14,)), dma((D // S * NT,)), dma((2,)), dma((2 * L,)), dma((2 * L,)),
                      dma((steps * (n_model - 1),)), dma((steps * (n_model - 1),)), dma((n_model - 1,)), dma((n_model - 1,)),
                      dma, dma])
        k_out, v_out, cand = pl.pallas_call(
            functools.partial(decode_kernel, cfg),
            out_shape=(jax.ShapeDtypeStruct((L, B, C, S), BF16), jax.ShapeDtypeStruct((L, B, C, S), BF16),
                       jax.ShapeDtypeStruct((B, V), F32)),
            in_specs=[sm, sm, vm, vm, vm, vm, vm, vm, vm, vm] + [any_spec] * 10,
            out_specs=(any_spec, any_spec, vm),
            scratch_shapes=scratch,
            compiler_params=pltpu.CompilerParams(collective_id=0, has_side_effects=True, vmem_limit_bytes=64 * 1024 * 1024 - 65536),
            name="decode_step",
        )(rows, position.reshape(1), x_embed, jnp.broadcast_to(rows[:, None], (B, 128)), score_pad, cos, sin, gain_attn, gain_mlp,
          gain_final[None], flat(k_cache), flat(v_cache), w_query, w_key, w_value, w_out, w_gate, w_up, w_down, w_vocab.T)
        back = lambda c: jnp.transpose(c.reshape(L, B, KH, HD, S), (0, 1, 4, 2, 3))
        return back(k_out), back(v_out), cand

    return jax.shard_map(local_step, mesh=mesh, in_specs=in_specs, out_specs=out_specs, check_vma=False)
```

time: 601 us -> 119 us (0.20)
  waiting for transfers between devices: 251 us -> 0 us
  local copies, waits for them, and re-layouts: 160 us -> 23 us
  Pallas kernels: 0 us -> 94 us
  other arithmetic: 85.6 us -> 0.13 us
  matrix products: 58.2 us -> 0 us
  blocking collectives: 24.5 us -> 0 us
  between operations: 16 us -> 1.32 us
    psum x8 -> x0, waiting for transfers between devices: 250 us -> none  [the longest x4 127 us: layer_body(): lax.psum(jnp.dot(hidden, w_down, preferred_element_type=jnp.float32), 'mo...]
    pallas_call x0 -> x1, Pallas kernels: none -> 94 us  [local_step(): pl.pallas_call(functools.partial(decode_kernel, cfg), out_shape=(jax.Shap...]
    dynamic_update_slice x8 -> x0, local copies, waits for them, and re-layouts: 65.4 us -> none  [the longest x4 33.6 us: layer_body(): v_sel = lax.dynamic_update_slice(v_sel, v_new[:, None], (0, position, 0, 0))]
    gather x17 -> x0, local copies, waits for them, and re-layouts: 60.9 us -> none  [the longest x8 33.8 us: reorder(): return jnp.take(jnp.concatenate(pooled, axis=0), pick_index, axis=0)]
    dot_general x33 -> x0, matrix products: 58.2 us -> none  [the longest x4 14.4 us: layer_body(): jnp.dot(hidden, w_down, preferred_element_type=jnp.float32)]
    concatenate x16 -> x0, other arithmetic: 36.8 us -> none  [the longest x8 36.1 us: reorder(): return jnp.take(jnp.concatenate(pooled, axis=0), pick_index, axis=0)]
    select_n x4 -> x0, other arithmetic: 23.1 us -> none  [the longest x1 12.3 us: reorder(): outgoing = jnp.take(cache_layer, send_index[step_idx], axis=0)]
    unnamed x47 -> x7, local copies, waits for them, and re-layouts: 0.92 us -> 17.7 us
  transfers between devices with their start and end apart: 16 -> 0, of which waited for: 9 -> 0; matrix products, arithmetic and copies ran while one was open for 15% -> 0% of each run, Pallas kernels for 0% -> 0%
where the time goes in v1:
time: 119 us; the launch traced here: 118 us
  Pallas kernels  94 us (79%)
  local copies, waits for them, and re-layouts  23 us (19%)
  between operations  1.32 us (1%)
    pallas_call x1, Pallas kernels, local_step(): pl.pallas_call(functools.partial(decode_kernel, cfg), out_shape=(jax.Shap...  94 us
    unnamed x7, local copies, waits for them, and re-layouts  17.7 us

profile of v1, /device:TPU:0, one launch (start us, length us, event | category | flops | bytes accessed | tf_op | source)
XLA Modules:
  0.0 118.4 jit_solution(8785844938136964826)
XLA Ops:
  1.3 0.8 reshape.37
  2.0 0.1 dynamic-slice_subtract_fusion.refs_0_
  2.1 0.0 copy-start.1
  2.1 0.7 pad.4
  2.9 0.7 broadcast_in_dim_tile.7.refs_6_
  3.5 0.6 broadcast_in_dim.7.refs_4_
  4.1 0.7 broadcast_in_dim_tile.6.refs_5_
  4.8 1.3 %broadcast_in_dim.8.refs_9_ = bf16[1,1024]{1,0:T(2,128)(2,1)} reshape(bf16[1024]{0:T(1024)(128)(2,1)} %param.32) | data formatting | bytes 4096 | tf_op jit(solution)/shard_map/broadcast_in_dim | solution.py:317
  6.0 0.0 copy-done.1
  6.0 0.7 broadcast_in_dim.6.refs_3_
  6.7 94.0 %decode_step.1 = (bf16[4,16,256,256]{3,2,1,0:T(8,128)(2,1)}, bf16[4,16,256,256]{3,2,1,0:T(8,128)(2,1)}, f32[16,8032]{1,0:T(8,128)}) custom-call(s32[16]{0:T(128)} %copy-done.1, s32[1]{0:T(128)} %bitcast.14.refs_1_, bf16[16,1024]{1,0:T(8,128)(2,1)} %refs_2_.1, s32[16,128]{1,0:T(8,128)} %broadcast_in_dim.6.refs_3_, f32[8,128]{1,0:T(8,128)} %broadcast_in_dim.7.refs_4_, ...), custom_call_target="tpu_custom_call" | custom-call | tf_op jit(solution)/shard_map/decode_step/pallas_call | solution.py:307
  100.7 8.4 %copy.24 = bf16[4,16,256,4,64]{2,4,3,1,0:T(8,128)(2,1)} copy(bf16[4,16,256,4,64]{2,4,3,1,0:T(8,128)(2,1)} %bitcast.17) | data formatting | bytes 16777216
  109.1 0.0 copy-start
  109.1 8.5 %copy.25 = bf16[4,16,256,4,64]{2,4,3,1,0:T(8,128)(2,1)} copy(bf16[4,16,256,4,64]{2,4,3,1,0:T(8,128)(2,1)} %bitcast.16) | data formatting | bytes 16777216
  117.6 0.0 copy-done
  117.6 0.8 copy.26
  (3 shorter events, 0.1 us)
Async XLA Ops:
  2.1 3.9 %copy-start.1 = (s32[16]{0:T(128)}, s32[16]{0:T(128)S(1)}, u32[]{:S(2)}) copy-start(s32[16]{0:T(128)S(1)} %dynamic-slice_subtract_fusion.refs_0_) | copy-start | bytes 196
  109.1 8.5 %copy-start = (f32[16,8032]{1,0:T(8,128)S(1)}, f32[16,8032]{1,0:T(8,128)}, u32[]{:S(2)}) copy-start(f32[16,8032]{1,0:T(8,128)} %get-tuple-element.16) | copy-start | bytes 1542148

commit v2 on v1

v2 whole, which is shorter than its diff:
```python
import functools

import jax
import jax.numpy as jnp
import numpy as np
from jax import lax
from jax.experimental import pallas as pl
from jax.experimental.pallas import tpu as pltpu
from jax.sharding import PartitionSpec as P

NORM_EPS = 1e-6
ROPE_BASE = 10000.0
MESH = pl.DeviceIdType.MESH
F32 = jnp.float32
BF16 = jnp.bfloat16
LANES = 128
SUB = 8


def rms(res, gain):
    inv = lax.rsqrt(jnp.mean(res * res, axis=-1, keepdims=True) + NORM_EPS)
    return (res * inv * gain.astype(F32)).astype(BF16)


def dot(a, b):
    return jnp.dot(a, b, preferred_element_type=F32)


def dot_t(a, b):
    return lax.dot_general(a, b, (((1,), (1,)), ((), ())), preferred_element_type=F32)


def decode_kernel(cfg, *refs):
    L, B, D, HD, S, KH, FF, V, NM, SPAN = cfg
    (parent_ref, pos_ref, x_ref, score_ref, freq_ref, ga_ref, gm_ref, gf_ref,
     kc, vc, wq, wk, wv, wo, wg, wu, wd, wt, kst, vst, cand_ref,
     kb0, kb1, vb0, vb1, wqb, wkb, wvb, wob, wgb, wub, wdb, ar, stat, scb, res, qs, lg, pr, osc, lgt,
     sem_c, sem_w, sem_t, free, bsend, brecv, asend, arecv, ssend, srecv, csend, crecv) = refs
    kb = (kb0, kb1)
    vb = (vb0, vb1)
    C = KH * HD
    me = lax.axis_index("model")
    beam = lax.axis_index("beam")
    spos = lax.rem(beam, SPAN)
    sent = lax.div(beam, SPAN)
    partner = beam - spos + lax.rem(spos + 1, SPAN)
    own = pl.ds(spos * B, B)

    def cache_local(l):
        return (pltpu.make_async_copy(kc.at[l], kb[l % 2].at[own], sem_c.at[2 * l]),
                pltpu.make_async_copy(vc.at[l], vb[l % 2].at[own], sem_c.at[2 * l + 1]))

    def cache_push(l):
        return tuple(pltpu.make_async_remote_copy(src_ref=c.at[l], dst_ref=buf[l % 2].at[own], send_sem=bsend.at[2 * l + i],
                                                  recv_sem=brecv.at[2 * l + i], device_id={"beam": partner}, device_id_type=MESH)
                     for i, (c, buf) in enumerate(((kc, kb), (vc, vb))))

    weights = ((wq, wqb), (wk, wkb), (wv, wvb), (wo, wob), (wg, wgb), (wu, wub), (wd, wdb))

    def weight(l, i):
        src, buf = weights[i]
        return pltpu.make_async_copy(src.at[l], buf.at[l % 2], sem_w.at[(l % 2) * 7 + i])

    chunks = (kb0, vb0, kb1, vb1)
    NCH = D // S
    NT = lgt.shape[0]
    TN = lgt.shape[2]

    def vocab(c, n, rows=TN):
        start = n * TN if isinstance(n, int) else pl.multiple_of(n * TN, TN)
        return pltpu.make_async_copy(wt.at[pl.ds(start, rows), c * S:(c + 1) * S], chunks[c].at[n, pl.ds(0, rows)],
                                     sem_t.at[c * NT + n])

    def vocab_all(which, act):
        def body(n, carry):
            for c in which:
                act(vocab(c, n))
            return carry
        full = V // TN
        lax.fori_loop(0, full, body, 0)
        if full < NT:
            for c in which:
                act(vocab(c, full, V - full * TN))

    for i in range(3):
        weight(0, i).start()
    for c in cache_local(0):
        c.start()

    barrier = pltpu.get_barrier_semaphore()
    for k in range(1, NM):
        pl.semaphore_signal(barrier, inc=1, device_id={"model": lax.rem(me + k, NM)}, device_id_type=MESH)
    pl.semaphore_signal(barrier, inc=1, device_id={"beam": partner}, device_id_type=MESH)

    scb[0] = jnp.zeros((SUB, LANES), F32)
    scb[0, 0:1, 0:B] = score_ref[...]
    pos = pos_ref[0]
    angle = pos.astype(F32) * freq_ref[...]
    cos = jnp.cos(angle)
    sin = jnp.sin(angle)
    low = lax.rem(lax.broadcasted_iota(jnp.int32, (B, C), 1), HD) < HD // 2
    rows = [lax.rem(parent_ref[sent, spos * B + b], SPAN * B) for b in range(B)]

    pl.semaphore_wait(barrier, NM)

    for c in cache_push(0):
        c.start()
    score_copy = pltpu.make_async_remote_copy(src_ref=scb.at[0], dst_ref=scb.at[1], send_sem=csend, recv_sem=crecv,
                                              device_id={"beam": partner}, device_id_type=MESH)
    score_copy.start()
    for i in range(3, 7):
        weight(0, i).start()
    for i in range(7):
        weight(1, i).start()

    def reduce_copies(step):
        slot = step * NM + me
        return [pltpu.make_async_remote_copy(src_ref=ar.at[slot], dst_ref=ar.at[slot], send_sem=asend.at[step * (NM - 1) + k - 1],
                                             recv_sem=arecv.at[step * (NM - 1) + k - 1],
                                             device_id={"model": lax.rem(me + k, NM)}, device_id_type=MESH)
                for k in range(1, NM)]

    def reduce_start(step, value):
        ar[step * NM + me] = value
        copies = reduce_copies(step)
        for c in copies:
            c.start()
        return copies

    def reduce_finish(step, copies):
        for c in copies:
            c.wait_recv()
        total = ar[step * NM]
        for k in range(1, NM):
            total = total + ar[step * NM + k]
        return total

    def rope(x):
        other = jnp.where(low, -pltpu.roll(x, C - HD // 2, 1), pltpu.roll(x, HD // 2, 1))
        return x * cos + other * sin

    head_of_lane = lax.broadcasted_iota(jnp.int32, (SUB, C), 1) // HD
    head_mask = head_of_lane == lax.broadcasted_iota(jnp.int32, (SUB, C), 0)
    here = lax.broadcasted_iota(jnp.int32, (C, S), 1) == pos
    res[...] = x_ref[...].astype(F32)
    sends = [score_copy]

    for l in range(L):
        ws = l % 2
        h = rms(res[...], ga_ref[l:l + 1, :])
        for i in range(3):
            weight(l, i).wait()
        q = rope(dot(h, wqb[ws])).astype(BF16).astype(F32)
        k = rope(dot(h, wkb[ws])).astype(BF16).astype(F32)
        v = dot(h, wvb[ws]).astype(BF16).astype(F32)
        qs[...] = q * (HD ** -0.5)
        pad = jnp.zeros((LANES - B, C), F32)
        k_cols = jnp.concatenate([k, pad], axis=0).T
        v_cols = jnp.concatenate([v, pad], axis=0).T
        for c in cache_local(l):
            c.wait()
        pushes = cache_push(l)
        sends += list(pushes)
        pushes[0].wait_recv()
        for b in range(B):
            kept = jnp.where(here, jnp.broadcast_to(k_cols[:, b:b + 1], (C, S)).astype(BF16), kb[ws][rows[b]])
            kst[l, b] = kept
            qb = jnp.where(head_mask, jnp.broadcast_to(qs[b:b + 1, :], (SUB, C)), 0.0).astype(BF16)
            lg[b * SUB:(b + 1) * SUB, :] = dot(qb, kept)
        logits = lg[...]
        logits = jnp.where(lax.broadcasted_iota(jnp.int32, logits.shape, 1) <= pos, logits, -jnp.inf)
        e = jnp.exp(logits - jnp.max(logits, axis=-1, keepdims=True))
        pr[...] = e / jnp.sum(e, axis=-1, keepdims=True)
        pushes[1].wait_recv()
        for b in range(B):
            kept = jnp.where(here, jnp.broadcast_to(v_cols[:, b:b + 1], (C, S)).astype(BF16), vb[ws][rows[b]])
            vst[l, b] = kept
            ob = dot_t(pr[b * SUB:(b + 1) * SUB, :].astype(BF16), kept)
            osc[b:b + 1, :] = jnp.sum(jnp.where(head_mask, ob, 0.0), axis=0, keepdims=True)
        if l + 2 < L:
            pl.semaphore_signal(free, inc=1, device_id={"beam": partner}, device_id_type=MESH)
        weight(l, 3).wait()
        copies = reduce_start(2 * l, dot(osc[...].astype(BF16), wob[ws]))
        sends += copies
        if l + 1 < L:
            for c in cache_local(l + 1):
                c.start()
            if l + 1 >= 2:
                pl.semaphore_wait(free, 1)
            for c in cache_push(l + 1):
                c.start()
            if l + 2 < L:
                for i in range(4):
                    weight(l + 2, i).start()
        if l == L - 1:
            vocab_all(range(NCH), lambda c: c.start())
        r = res[...] + reduce_finish(2 * l, copies)
        h = rms(r, gm_ref[l:l + 1, :])
        weight(l, 4).wait()
        weight(l, 5).wait()
        gate = dot(h, wgb[ws])
        up = dot(h, wub[ws])
        g = (gate * jax.nn.sigmoid(gate) * up).astype(BF16)
        weight(l, 6).wait()
        copies = reduce_start(2 * l + 1, dot(g, wdb[ws]))
        sends += copies
        if l + 2 < L:
            for i in range(4, 7):
                weight(l + 2, i).start()
        res[...] = r + reduce_finish(2 * l + 1, copies)

    gf = gf_ref[...].astype(F32)
    h = rms(res[...], jnp.concatenate([gf[i:i + 1, :] for i in range(D // LANES)], axis=1))
    vocab_all(range(NCH), lambda c: c.wait())

    def tile(n, carry):
        acc = dot_t(h[:, 0:S], chunks[0][n])
        for c in range(1, NCH):
            acc = acc + dot_t(h[:, c * S:(c + 1) * S], chunks[c][n])
        acc = jnp.where(lax.broadcasted_iota(jnp.int32, (B, TN), 1) + n * TN < V, acc, -jnp.inf)
        lgt[n] = acc
        return jnp.maximum(carry, acc)

    peak = lax.fori_loop(0, NT, tile, jnp.full((B, TN), -jnp.inf, F32))
    m = jnp.max(peak, axis=-1, keepdims=True)

    def add_exp(n, carry):
        return carry + jnp.exp(lgt[n] - m)

    s = jnp.sum(lax.fori_loop(0, NT, add_exp, jnp.zeros((B, TN), F32)), axis=-1, keepdims=True)
    stat[me, 0] = jnp.broadcast_to(m, (B, LANES))
    stat[me, 1] = jnp.broadcast_to(s, (B, LANES))
    copies = [pltpu.make_async_remote_copy(src_ref=stat.at[me], dst_ref=stat.at[me], send_sem=ssend.at[k - 1], recv_sem=srecv.at[k - 1],
                                           device_id={"model": lax.rem(me + k, NM)}, device_id_type=MESH) for k in range(1, NM)]
    for c in copies:
        c.start()
    sends += copies
    score_copy.wait_recv()
    sub = lax.broadcasted_iota(jnp.int32, (B, LANES), 0)
    want = jnp.zeros((B, LANES), jnp.int32)
    for b in range(B):
        want = jnp.where(sub == b, rows[b], want)
    lane = lax.broadcasted_iota(jnp.int32, (B, LANES), 1)
    mine = jnp.where(lane + spos * B == want, scb[0, 0:1, :], 0.0)
    theirs = jnp.where(lane + (SPAN - 1 - spos) * B == want, scb[1, 0:1, :], 0.0)
    parent_score = jnp.sum(jnp.where(lane < B, mine + theirs, 0.0), axis=-1, keepdims=True)
    for c in copies:
        c.wait_recv()
    gm = stat[0, 0]
    for k in range(1, NM):
        gm = jnp.maximum(gm, stat[k, 0])
    gs = stat[0, 1] * jnp.exp(stat[0, 0] - gm)
    for k in range(1, NM):
        gs = gs + stat[k, 1] * jnp.exp(stat[k, 0] - gm)
    gm = gm[:, 0:1]
    log_s = jnp.log(gs)[:, 0:1]
    for n in range(NT):
        hi = min((n + 1) * TN, V)
        cand_ref[:, n * TN:hi] = parent_score + ((lgt[n] - gm) - log_s)[:, :hi - n * TN]
    for c in sends:
        c.wait_send()


def write_kernel(*refs):
    n = (len(refs) - 1) // 2
    sem = refs[-1]
    copies = []
    for i in range(n):
        src, dst = refs[i], refs[n + i]
        if len(src.shape) > 2:
            copies += [(src.at[j], dst.at[j]) for j in range(src.shape[0])]
        else:
            copies.append((src, dst))
    copies = [pltpu.make_async_copy(a, b, sem.at[j]) for j, (a, b) in enumerate(copies)]
    for c in copies:
        c.start()
    for c in copies:
        c.wait()


def solution(mesh):
    data_beam = ('data', 'beam')
    cache_spec = P(None, data_beam, None, 'model', None)
    col_spec = P(None, None, 'model')
    row_spec = P(None, 'model', None)
    in_specs = (P(data_beam, None), P('data', None), P(), P(data_beam), cache_spec, cache_spec,
                P(), col_spec, col_spec, col_spec, row_spec, P(), col_spec, col_spec, row_spec, P(), P(None, 'model'))
    out_specs = (cache_spec, cache_spec, P(data_beam, 'model'))
    n_model = mesh.shape['model']

    def local_step(x_embed, parent, position, score, k_cache, v_cache, gain_attn, w_query, w_key, w_value, w_out, gain_mlp,
                   w_gate, w_up, w_down, gain_final, w_vocab):
        L, B, S, KH, HD = k_cache.shape
        D = x_embed.shape[1]
        C = KH * HD
        FF = w_gate.shape[2]
        V = w_vocab.shape[1]
        span = parent.shape[1] // B
        half = HD // 2
        freq = np.power(ROPE_BASE, -(np.arange(half, dtype=np.float64) / half)).astype(np.float32)
        freq = jnp.asarray(np.tile(freq, 2 * KH)[None])
        flat = lambda c: jnp.transpose(c, (0, 1, 3, 4, 2)).reshape(L, B, C, S)
        cfg = (L, B, D, HD, S, KH, FF, V, n_model, span)
        any_spec = pl.BlockSpec(memory_space=pl.ANY)
        vm = pl.BlockSpec(memory_space=pltpu.VMEM)
        sm = pl.BlockSpec(memory_space=pltpu.SMEM)
        steps = 2 * L
        TN = C
        NT = -(-V // TN)
        dma = pltpu.SemaphoreType.DMA
        cache_shape = (L, B, C, S)
        scratch = ([pltpu.VMEM((span * B, C, S), BF16) for _ in range(4)]
                   + [pltpu.VMEM((2, D, C), BF16)] * 3 + [pltpu.VMEM((2, C, D), BF16)]
                   + [pltpu.VMEM((2, D, FF), BF16)] * 2 + [pltpu.VMEM((2, FF, D), BF16)]
                   + [pltpu.VMEM((steps * n_model, B, D), F32), pltpu.VMEM((n_model, 2, B, LANES), F32), pltpu.VMEM((2, SUB, LANES), F32),
                      pltpu.VMEM((B, D), F32), pltpu.VMEM((B, C), F32), pltpu.VMEM((B * SUB, S), F32), pltpu.VMEM((B * SUB, S), F32),
                      pltpu.VMEM((B, C), F32), pltpu.VMEM((NT, B, TN), F32),
                      dma((2 * L,)), dma((14,)), dma((D // S * NT,)), pltpu.SemaphoreType.REGULAR, dma((2 * L,)), dma((2 * L,)),
                      dma((steps * (n_model - 1),)), dma((steps * (n_model - 1),)), dma((n_model - 1,)), dma((n_model - 1,)),
                      dma, dma])
        limit = 64 * 1024 * 1024 - 65536
        outs = pl.pallas_call(
            functools.partial(decode_kernel, cfg),
            out_shape=(pltpu.VMEM(cache_shape, BF16), pltpu.VMEM(cache_shape, BF16), pltpu.VMEM((B, V), F32)),
            in_specs=[sm, sm, vm, vm, vm, vm, vm, vm] + [any_spec] * 10,
            out_specs=(vm, vm, vm),
            scratch_shapes=scratch,
            compiler_params=pltpu.CompilerParams(collective_id=0, has_side_effects=True,
                                                 vmem_limit_bytes=limit - 2 * L * B * C * S * 2 - B * (V + LANES) * 4 - (1 << 19)),
            name="decode_step",
        )(parent, position.reshape(1), x_embed, score[None], freq, gain_attn, gain_mlp, gain_final.reshape(D // LANES, LANES),
          flat(k_cache), flat(v_cache), w_query, w_key, w_value, w_out, w_gate, w_up, w_down, w_vocab.T)
        k_out, v_out, cand = pl.pallas_call(
            write_kernel,
            out_shape=(jax.ShapeDtypeStruct(cache_shape, BF16), jax.ShapeDtypeStruct(cache_shape, BF16),
                       jax.ShapeDtypeStruct((B, V), F32)),
            in_specs=[vm, vm, vm],
            out_specs=(any_spec, any_spec, any_spec),
            scratch_shapes=[dma((2 * L + 1,))],
            compiler_params=pltpu.CompilerParams(vmem_limit_bytes=1 << 20),
            name="write_out",
        )(*outs)
        back = lambda c: jnp.transpose(c.reshape(L, B, KH, HD, S), (0, 1, 4, 2, 3))
        return back(k_out), back(v_out), cand

    return jax.shard_map(local_step, mesh=mesh, in_specs=in_specs, out_specs=out_specs, check_vma=False)
```

time: 119 us -> 101 us (0.85)
  local copies, waits for them, and re-layouts: 23 us -> 0 us
  Pallas kernels: 94 us -> 99.3 us
    unnamed x7 -> x0, local copies, waits for them, and re-layouts: 17.7 us -> none
    pallas_call x1 -> x2, Pallas kernels: 94 us -> 99.3 us  [the longest x1 93.2 us: local_step(): pl.pallas_call(functools.partial(decode_kernel, cfg), out_shape=(pltpu.VM...]
    broadcast_in_dim x3 -> x0, local copies, waits for them, and re-layouts: 2.54 us -> none  [the longest x1 1.28 us: local_step(): gain_final[None]]
    another operation x4 -> x0, local copies, waits for them, and re-layouts: 1.32 us -> none  [the longest x2 0.66 us: local_step(): sin = jnp.tile(jnp.sin(angles), 2 * KH)[None]]
where the time goes in v2:
time: 101 us
  Pallas kernels  99.3 us (98%)
  between operations  1.29 us (1%)
    pallas_call x1, Pallas kernels, local_step(): pl.pallas_call(functools.partial(decode_kernel, cfg), out_shape=(pltpu.VM...  93.2 us
    pallas_call x1, Pallas kernels, local_step(): pl.pallas_call(write_kernel, out_shape=(jax.ShapeDtypeStruct(cache_shape,...  6.03 us

profile of v2, /device:TPU:0, one launch (start us, length us, event | category | flops | bytes accessed | tf_op | source)
XLA Modules:
  0.0 100.5 jit_solution(1194822323020739666)
XLA Ops:
  1.3 93.2 %decode_step.1 = (bf16[4,16,256,256]{3,2,1,0:T(8,128)(2,1)S(1)}, bf16[4,16,256,256]{3,2,1,0:T(8,128)(2,1)S(1)}, f32[16,8032]{1,0:T(8,128)S(1)}) custom-call(s32[2,32]{1,0:T(2,128)} %refs_0_.1, s32[1]{0:T(128)} %bitcast.16.refs_1_, bf16[16,1024]{1,0:T(8,128)(2,1)} %refs_2_.1, f32[1,16]{1,0:T(1,128)} %bitcast.21, f32[1,256]{1,0:T(1,128)} %constant.2.clone.refs_4_, ...), custom_call_target="tpu_custom_call" | custom-call | tf_op jit(solution)/shard_map/decode_step/pallas_call | solution.py:322
  94.5 6.0 %write_out.1 = (bf16[4,16,256,256]{3,2,1,0:T(8,128)(2,1)}, bf16[4,16,256,256]{3,2,1,0:T(8,128)(2,1)}, f32[16,8032]{1,0:T(8,128)}) custom-call(bf16[4,16,256,256]{3,2,1,0:T(8,128)(2,1)S(1)} %get-tuple-element.9.refs_0_, bf16[4,16,256,256]{3,2,1,0:T(8,128)(2,1)S(1)} %get-tuple-element.10.refs_1_, f32[16,8032]{1,0:T(8,128)S(1)} %get-tuple-element.11.refs_2_), custom_call_target="tpu_custom_call" | custom-call | tf_op jit(solution)/shard_map/write_out/pallas_call | solution.py:333

commit v3 on v2

--- a/solution.py
+++ b/solution.py
@@ -39,6 +39,7 @@
     kb = (kb0, kb1)
     vb = (vb0, vb1)
     C = KH * HD
+    NH, HB = res.shape[:2]
     me = lax.axis_index("model")
     beam = lax.axis_index("beam")
     spos = lax.rem(beam, SPAN)
@@ -98,7 +99,7 @@
     angle = pos.astype(F32) * freq_ref[...]
     cos = jnp.cos(angle)
     sin = jnp.sin(angle)
-    low = lax.rem(lax.broadcasted_iota(jnp.int32, (B, C), 1), HD) < HD // 2
+    low = lax.rem(lax.broadcasted_iota(jnp.int32, (HB, C), 1), HD) < HD // 2
     rows = [lax.rem(parent_ref[sent, spos * B + b], SPAN * B) for b in range(B)]
 
     pl.semaphore_wait(barrier, NM)
@@ -113,21 +114,24 @@
     for i in range(7):
         weight(1, i).start()
 
-    def reduce_copies(step):
+    def peers():
+        if NM == 4:
+            return [(3, NM - 1 - me), (2, lax.rem(me + 2, NM)), (1, me + 1 - 2 * lax.rem(me, 2))]
+        return [(k, lax.rem(me + k, NM)) for k in range(1, NM)]
+
+    def reduce_start(step, value):
         slot = step * NM + me
-        return [pltpu.make_async_remote_copy(src_ref=ar.at[slot], dst_ref=ar.at[slot], send_sem=asend.at[step * (NM - 1) + k - 1],
-                                             recv_sem=arecv.at[step * (NM - 1) + k - 1],
-                                             device_id={"model": lax.rem(me + k, NM)}, device_id_type=MESH)
-                for k in range(1, NM)]
-
-    def reduce_start(step, value):
-        ar[step * NM + me] = value
-        copies = reduce_copies(step)
+        ar[slot] = value
+        copies = [pltpu.make_async_remote_copy(src_ref=ar.at[slot], dst_ref=ar.at[slot], send_sem=asend.at[step * (NM - 1) + k - 1],
+                                               recv_sem=arecv.at[step * (NM - 1) + k - 1],
+                                               device_id={"model": peer}, device_id_type=MESH) for k, peer in peers()]
         for c in copies:
             c.start()
-        return copies
-
-    def reduce_finish(step, copies):
+        sends.extend(copies)
+        return step, copies
+
+    def reduce_finish(started):
+        step, copies = started
         for c in copies:
             c.wait_recv()
         total = ar[step * NM]
@@ -142,75 +146,96 @@
     head_of_lane = lax.broadcasted_iota(jnp.int32, (SUB, C), 1) // HD
     head_mask = head_of_lane == lax.broadcasted_iota(jnp.int32, (SUB, C), 0)
     here = lax.broadcasted_iota(jnp.int32, (C, S), 1) == pos
-    res[...] = x_ref[...].astype(F32)
     sends = [score_copy]
-
-    for l in range(L):
+    pushes = [cache_push(0)]
+    sends.extend(pushes[0])
+
+    def attend(l, i, r):
         ws = l % 2
-        h = rms(res[...], ga_ref[l:l + 1, :])
-        for i in range(3):
-            weight(l, i).wait()
+        h = rms(r, ga_ref[l:l + 1, :])
+        if i == 0:
+            for j in range(3):
+                weight(l, j).wait()
         q = rope(dot(h, wqb[ws])).astype(BF16).astype(F32)
         k = rope(dot(h, wkb[ws])).astype(BF16).astype(F32)
         v = dot(h, wvb[ws]).astype(BF16).astype(F32)
-        qs[...] = q * (HD ** -0.5)
-        pad = jnp.zeros((LANES - B, C), F32)
+        qs[i] = q * (HD ** -0.5)
+        pad = jnp.zeros((LANES - HB, C), F32)
         k_cols = jnp.concatenate([k, pad], axis=0).T
         v_cols = jnp.concatenate([v, pad], axis=0).T
-        for c in cache_local(l):
-            c.wait()
-        pushes = cache_push(l)
-        sends += list(pushes)
-        pushes[0].wait_recv()
-        for b in range(B):
-            kept = jnp.where(here, jnp.broadcast_to(k_cols[:, b:b + 1], (C, S)).astype(BF16), kb[ws][rows[b]])
-            kst[l, b] = kept
-            qb = jnp.where(head_mask, jnp.broadcast_to(qs[b:b + 1, :], (SUB, C)), 0.0).astype(BF16)
-            lg[b * SUB:(b + 1) * SUB, :] = dot(qb, kept)
-        logits = lg[...]
+        if i == 0:
+            cache_local(l)[0].wait()
+            pushes[l][0].wait_recv()
+        for b in range(HB):
+            kept = jnp.where(here, jnp.broadcast_to(k_cols[:, b:b + 1], (C, S)).astype(BF16), kb[ws][rows[i * HB + b]])
+            kst[l, i * HB + b] = kept
+            qb = jnp.where(head_mask, jnp.broadcast_to(qs[i, b:b + 1, :], (SUB, C)), 0.0).astype(BF16)
+            lg[i, b * SUB:(b + 1) * SUB, :] = dot(qb, kept)
+        logits = lg[i]
         logits = jnp.where(lax.broadcasted_iota(jnp.int32, logits.shape, 1) <= pos, logits, -jnp.inf)
         e = jnp.exp(logits - jnp.max(logits, axis=-1, keepdims=True))
-        pr[...] = e / jnp.sum(e, axis=-1, keepdims=True)
-        pushes[1].wait_recv()
-        for b in range(B):
-            kept = jnp.where(here, jnp.broadcast_to(v_cols[:, b:b + 1], (C, S)).astype(BF16), vb[ws][rows[b]])
-            vst[l, b] = kept
-            ob = dot_t(pr[b * SUB:(b + 1) * SUB, :].astype(BF16), kept)
-            osc[b:b + 1, :] = jnp.sum(jnp.where(head_mask, ob, 0.0), axis=0, keepdims=True)
-        if l + 2 < L:
-            pl.semaphore_signal(free, inc=1, device_id={"beam": partner}, device_id_type=MESH)
-        weight(l, 3).wait()
-        copies = reduce_start(2 * l, dot(osc[...].astype(BF16), wob[ws]))
-        sends += copies
-        if l + 1 < L:
-            for c in cache_local(l + 1):
-                c.start()
-            if l + 1 >= 2:
-                pl.semaphore_wait(free, 1)
-            for c in cache_push(l + 1):
-                c.start()
-            if l + 2 < L:
-                for i in range(4):
-                    weight(l + 2, i).start()
-        if l == L - 1:
-            vocab_all(range(NCH), lambda c: c.start())
-        r = res[...] + reduce_finish(2 * l, copies)
+        pr[i] = e / jnp.sum(e, axis=-1, keepdims=True)
+        if i == 0:
+            cache_local(l)[1].wait()
+            pushes[l][1].wait_recv()
+        for b in range(HB):
+            kept = jnp.where(here, jnp.broadcast_to(v_cols[:, b:b + 1], (C, S)).astype(BF16), vb[ws][rows[i * HB + b]])
+            vst[l, i * HB + b] = kept
+            ob = dot_t(pr[i, b * SUB:(b + 1) * SUB, :].astype(BF16), kept)
+            osc[i, b:b + 1, :] = jnp.sum(jnp.where(head_mask, ob, 0.0), axis=0, keepdims=True)
+        if i == 0:
+            weight(l, 3).wait()
+        return reduce_start(2 * l * NH + i, dot(osc[i].astype(BF16), wob[ws]))
+
+    def mlp(l, i, r):
+        ws = l % 2
         h = rms(r, gm_ref[l:l + 1, :])
-        weight(l, 4).wait()
-        weight(l, 5).wait()
+        if i == 0:
+            weight(l, 4).wait()
+            weight(l, 5).wait()
         gate = dot(h, wgb[ws])
         up = dot(h, wub[ws])
         g = (gate * jax.nn.sigmoid(gate) * up).astype(BF16)
-        weight(l, 6).wait()
-        copies = reduce_start(2 * l + 1, dot(g, wdb[ws]))
-        sends += copies
+        if i == 0:
+            weight(l, 6).wait()
+        return reduce_start((2 * l + 1) * NH + i, dot(g, wdb[ws]))
+
+    for i in range(NH):
+        res[i] = x_ref[i * HB:(i + 1) * HB, :].astype(F32)
+    started = [None] * NH
+    for l in range(L):
+        for i in range(NH):
+            if l > 0:
+                res[i] = res[i] + reduce_finish(started[i])
+            started[i] = attend(l, i, res[i])
         if l + 2 < L:
-            for i in range(4, 7):
-                weight(l + 2, i).start()
-        res[...] = r + reduce_finish(2 * l + 1, copies)
+            pl.semaphore_signal(free, inc=1, device_id={"beam": partner}, device_id_type=MESH)
+        if l + 1 < L:
+            if l + 1 >= 2:
+                pl.semaphore_wait(free, 1)
+            pushes.append(cache_push(l + 1))
+            sends.extend(pushes[l + 1])
+            pushes[l + 1][0].start()
+            for c in cache_local(l + 1):
+                c.start()
+        if l + 2 < L:
+            for j in range(4):
+                weight(l + 2, j).start()
+        if l == L - 1:
+            vocab_all(range(NCH), lambda c: c.start())
+        for i in range(NH):
+            res[i] = res[i] + reduce_finish(started[i])
+            started[i] = mlp(l, i, res[i])
+        if l + 1 < L:
+            pushes[l + 1][1].start()
+        if l + 2 < L:
+            for j in range(4, 7):
+                weight(l + 2, j).start()
+    for i in range(NH):
+        res[i] = res[i] + reduce_finish(started[i])
 
     gf = gf_ref[...].astype(F32)
-    h = rms(res[...], jnp.concatenate([gf[i:i + 1, :] for i in range(D // LANES)], axis=1))
+    h = rms(jnp.concatenate([res[i] for i in range(NH)], axis=0), jnp.concatenate([gf[i:i + 1, :] for i in range(D // LANES)], axis=1))
     vocab_all(range(NCH), lambda c: c.wait())
 
     def tile(n, carry):
@@ -305,6 +330,8 @@
         vm = pl.BlockSpec(memory_space=pltpu.VMEM)
         sm = pl.BlockSpec(memory_space=pltpu.SMEM)
         steps = 2 * L
+        NH = 2
+        HB = B // NH
         TN = C
         NT = -(-V // TN)
         dma = pltpu.SemaphoreType.DMA
@@ -312,11 +339,11 @@
         scratch = ([pltpu.VMEM((span * B, C, S), BF16) for _ in range(4)]
                    + [pltpu.VMEM((2, D, C), BF16)] * 3 + [pltpu.VMEM((2, C, D), BF16)]
                    + [pltpu.VMEM((2, D, FF), BF16)] * 2 + [pltpu.VMEM((2, FF, D), BF16)]
-                   + [pltpu.VMEM((steps * n_model, B, D), F32), pltpu.VMEM((n_model, 2, B, LANES), F32), pltpu.VMEM((2, SUB, LANES), F32),
-                      pltpu.VMEM((B, D), F32), pltpu.VMEM((B, C), F32), pltpu.VMEM((B * SUB, S), F32), pltpu.VMEM((B * SUB, S), F32),
-                      pltpu.VMEM((B, C), F32), pltpu.VMEM((NT, B, TN), F32),
+                   + [pltpu.VMEM((steps * NH * n_model, HB, D), F32), pltpu.VMEM((n_model, 2, B, LANES), F32), pltpu.VMEM((2, SUB, LANES), F32),
+                      pltpu.VMEM((NH, HB, D), F32), pltpu.VMEM((NH, HB, C), F32), pltpu.VMEM((NH, HB * SUB, S), F32),
+                      pltpu.VMEM((NH, HB * SUB, S), F32), pltpu.VMEM((NH, HB, C), F32), pltpu.VMEM((NT, B, TN), F32),
                       dma((2 * L,)), dma((14,)), dma((D // S * NT,)), pltpu.SemaphoreType.REGULAR, dma((2 * L,)), dma((2 * L,)),
-                      dma((steps * (n_model - 1),)), dma((steps * (n_model - 1),)), dma((n_model - 1,)), dma((n_model - 1,)),
+                      dma((steps * NH * (n_model - 1),)), dma((steps * NH * (n_model - 1),)), dma((n_model - 1,)), dma((n_model - 1,)),
                       dma, dma])
         limit = 64 * 1024 * 1024 - 65536
         outs = pl.pallas_call(

time: 101 us -> 91.6 us (0.907)
  Pallas kernels: 99.3 us -> 89.9 us
    pallas_call x1, Pallas kernels: 93.2 us -> 83.9 us  [local_step(): pl.pallas_call(functools.partial(decode_kernel, cfg), out_shape=(pltpu.VM...]
where the time goes in v3:
time: 91.6 us; the launch traced here: 91.4 us
  Pallas kernels  89.9 us (98%)
  between operations  1.45 us (2%)
    pallas_call x1, Pallas kernels, local_step(): pl.pallas_call(functools.partial(decode_kernel, cfg), out_shape=(pltpu.VM...  83.9 us
    pallas_call x1, Pallas kernels, local_step(): pl.pallas_call(write_kernel, out_shape=(jax.ShapeDtypeStruct(cache_shape,...  6.03 us

profile of v3, /device:TPU:0, one launch (start us, length us, event | category | flops | bytes accessed | tf_op | source)
XLA Modules:
  0.0 91.4 jit_solution(17914936785461265541)
XLA Ops:
  1.3 83.9 %decode_step.1 = (bf16[4,16,256,256]{3,2,1,0:T(8,128)(2,1)S(1)}, bf16[4,16,256,256]{3,2,1,0:T(8,128)(2,1)S(1)}, f32[16,8032]{1,0:T(8,128)S(1)}) custom-call(s32[2,32]{1,0:T(2,128)} %refs_0_.1, s32[1]{0:T(128)} %bitcast.16.refs_1_, bf16[16,1024]{1,0:T(8,128)(2,1)} %refs_2_.1, f32[1,16]{1,0:T(1,128)} %bitcast.21, f32[1,256]{1,0:T(1,128)} %constant.2.clone.refs_4_, ...), custom_call_target="tpu_custom_call" | custom-call | tf_op jit(solution)/shard_map/decode_step/pallas_call | solution.py:349
  85.2 6.0 %write_out.1 = (bf16[4,16,256,256]{3,2,1,0:T(8,128)(2,1)}, bf16[4,16,256,256]{3,2,1,0:T(8,128)(2,1)}, f32[16,8032]{1,0:T(8,128)}) custom-call(bf16[4,16,256,256]{3,2,1,0:T(8,128)(2,1)S(1)} %get-tuple-element.9.refs_0_, bf16[4,16,256,256]{3,2,1,0:T(8,128)(2,1)S(1)} %get-tuple-element.10.refs_1_, f32[16,8032]{1,0:T(8,128)S(1)} %get-tuple-element.11.refs_2_), custom_call_target="tpu_custom_call" | custom-call | tf_op jit(solution)/shard_map/write_out/pallas_call | solution.py:360

commit v4 on v3

--- a/solution.py
+++ b/solution.py
@@ -116,24 +116,26 @@
 
     def peers():
         if NM == 4:
-            return [(3, NM - 1 - me), (2, lax.rem(me + 2, NM)), (1, me + 1 - 2 * lax.rem(me, 2))]
-        return [(k, lax.rem(me + k, NM)) for k in range(1, NM)]
+            side = lax.div(me, 2)
+            return [3 - 3 * side, 2 - side, me + 1 - 2 * lax.rem(me, 2)]
+        return [lax.rem(me + k, NM) for k in range(1, NM)]
+
+    def reduce_copy(step, j, source, peer):
+        slot = step * NM + source
+        return pltpu.make_async_remote_copy(src_ref=ar.at[slot], dst_ref=ar.at[slot], send_sem=asend.at[step * (NM - 1) + j],
+                                            recv_sem=arecv.at[slot], device_id={"model": peer}, device_id_type=MESH)
 
     def reduce_start(step, value):
-        slot = step * NM + me
-        ar[slot] = value
-        copies = [pltpu.make_async_remote_copy(src_ref=ar.at[slot], dst_ref=ar.at[slot], send_sem=asend.at[step * (NM - 1) + k - 1],
-                                               recv_sem=arecv.at[step * (NM - 1) + k - 1],
-                                               device_id={"model": peer}, device_id_type=MESH) for k, peer in peers()]
+        ar[step * NM + me] = value
+        copies = [reduce_copy(step, j, me, peer) for j, peer in enumerate(peers())]
         for c in copies:
             c.start()
         sends.extend(copies)
-        return step, copies
-
-    def reduce_finish(started):
-        step, copies = started
-        for c in copies:
-            c.wait_recv()
+        return step
+
+    def reduce_finish(step):
+        for k in range(1, NM):
+            reduce_copy(step, 0, lax.rem(me + k, NM), me).wait_recv()
         total = ar[step * NM]
         for k in range(1, NM):
             total = total + ar[step * NM + k]
@@ -330,7 +332,7 @@
         vm = pl.BlockSpec(memory_space=pltpu.VMEM)
         sm = pl.BlockSpec(memory_space=pltpu.SMEM)
         steps = 2 * L
-        NH = 2
+        NH = 4
         HB = B // NH
         TN = C
         NT = -(-V // TN)
@@ -343,7 +345,7 @@
                       pltpu.VMEM((NH, HB, D), F32), pltpu.VMEM((NH, HB, C), F32), pltpu.VMEM((NH, HB * SUB, S), F32),
                       pltpu.VMEM((NH, HB * SUB, S), F32), pltpu.VMEM((NH, HB, C), F32), pltpu.VMEM((NT, B, TN), F32),
                       dma((2 * L,)), dma((14,)), dma((D // S * NT,)), pltpu.SemaphoreType.REGULAR, dma((2 * L,)), dma((2 * L,)),
-                      dma((steps * NH * (n_model - 1),)), dma((steps * NH * (n_model - 1),)), dma((n_model - 1,)), dma((n_model - 1,)),
+                      dma((steps * NH * (n_model - 1),)), dma((steps * NH * n_model,)), dma((n_model - 1,)), dma((n_model - 1,)),
                       dma, dma])
         limit = 64 * 1024 * 1024 - 65536
         outs = pl.pallas_call(

time: 91.6 us -> 92.1 us (level)
  no operation moved by 1% of the time
where the time goes in v4:
time: 92.1 us; the launch traced here: 91.9 us
  Pallas kernels  90.5 us (98%)
  between operations  1.47 us (2%)
    pallas_call x1, Pallas kernels, local_step(): pl.pallas_call(functools.partial(decode_kernel, cfg), out_shape=(pltpu.VM...  84.4 us
    pallas_call x1, Pallas kernels, local_step(): pl.pallas_call(write_kernel, out_shape=(jax.ShapeDtypeStruct(cache_shape,...  6.03 us

profile of v4, /device:TPU:0, one launch (start us, length us, event | category | flops | bytes accessed | tf_op | source)
XLA Modules:
  0.0 91.9 jit_solution(16994058071315590290)
XLA Ops:
  1.3 84.4 %decode_step.1 = (bf16[4,16,256,256]{3,2,1,0:T(8,128)(2,1)S(1)}, bf16[4,16,256,256]{3,2,1,0:T(8,128)(2,1)S(1)}, f32[16,8032]{1,0:T(8,128)S(1)}) custom-call(s32[2,32]{1,0:T(2,128)} %refs_0_.1, s32[1]{0:T(128)} %bitcast.16.refs_1_, bf16[16,1024]{1,0:T(8,128)(2,1)} %refs_2_.1, f32[1,16]{1,0:T(1,128)} %bitcast.21, f32[1,256]{1,0:T(1,128)} %constant.2.clone.refs_4_, ...), custom_call_target="tpu_custom_call" | custom-call | tf_op jit(solution)/shard_map/decode_step/pallas_call | solution.py:351
  85.7 6.0 %write_out.1 = (bf16[4,16,256,256]{3,2,1,0:T(8,128)(2,1)}, bf16[4,16,256,256]{3,2,1,0:T(8,128)(2,1)}, f32[16,8032]{1,0:T(8,128)}) custom-call(bf16[4,16,256,256]{3,2,1,0:T(8,128)(2,1)S(1)} %get-tuple-element.9.refs_0_, bf16[4,16,256,256]{3,2,1,0:T(8,128)(2,1)S(1)} %get-tuple-element.10.refs_1_, f32[16,8032]{1,0:T(8,128)S(1)} %get-tuple-element.11.refs_2_), custom_call_target="tpu_custom_call" | custom-call | tf_op jit(solution)/shard_map/write_out/pallas_call | solution.py:362

commit v5 on v4

--- a/solution.py
+++ b/solution.py
@@ -85,8 +85,9 @@
 
     for i in range(3):
         weight(0, i).start()
-    for c in cache_local(0):
-        c.start()
+    for l in range(2):
+        for c in cache_local(l):
+            c.start()
 
     barrier = pltpu.get_barrier_semaphore()
     for k in range(1, NM):
@@ -104,7 +105,8 @@
 
     pl.semaphore_wait(barrier, NM)
 
-    for c in cache_push(0):
+    pushes = [cache_push(l) for l in range(L)]
+    for c in (pushes[0][0], pushes[0][1], pushes[1][0]):
         c.start()
     score_copy = pltpu.make_async_remote_copy(src_ref=scb.at[0], dst_ref=scb.at[1], send_sem=csend, recv_sem=crecv,
                                               device_id={"beam": partner}, device_id_type=MESH)
@@ -149,8 +151,7 @@
     head_mask = head_of_lane == lax.broadcasted_iota(jnp.int32, (SUB, C), 0)
     here = lax.broadcasted_iota(jnp.int32, (C, S), 1) == pos
     sends = [score_copy]
-    pushes = [cache_push(0)]
-    sends.extend(pushes[0])
+    sends.extend(pushes[l][i] for l in range(L) for i in range(2))
 
     def attend(l, i, r):
         ws = l % 2
@@ -212,14 +213,10 @@
             started[i] = attend(l, i, res[i])
         if l + 2 < L:
             pl.semaphore_signal(free, inc=1, device_id={"beam": partner}, device_id_type=MESH)
+            for c in cache_local(l + 2):
+                c.start()
         if l + 1 < L:
-            if l + 1 >= 2:
-                pl.semaphore_wait(free, 1)
-            pushes.append(cache_push(l + 1))
-            sends.extend(pushes[l + 1])
-            pushes[l + 1][0].start()
-            for c in cache_local(l + 1):
-                c.start()
+            pushes[l + 1][1].start()
         if l + 2 < L:
             for j in range(4):
                 weight(l + 2, j).start()
@@ -228,9 +225,9 @@
         for i in range(NH):
             res[i] = res[i] + reduce_finish(started[i])
             started[i] = mlp(l, i, res[i])
-        if l + 1 < L:
-            pushes[l + 1][1].start()
         if l + 2 < L:
+            pl.semaphore_wait(free, 1)
+            pushes[l + 2][0].start()
             for j in range(4, 7):
                 weight(l + 2, j).start()
     for i in range(NH):
@@ -295,7 +292,7 @@
     for i in range(n):
         src, dst = refs[i], refs[n + i]
         if len(src.shape) > 2:
-            copies += [(src.at[j], dst.at[j]) for j in range(src.shape[0])]
+            copies += [(src.at[j, k], dst.at[j, k]) for j in range(src.shape[0]) for k in range(src.shape[1])]
         else:
             copies.append((src, dst))
     copies = [pltpu.make_async_copy(a, b, sem.at[j]) for j, (a, b) in enumerate(copies)]
@@ -365,7 +362,7 @@
                        jax.ShapeDtypeStruct((B, V), F32)),
             in_specs=[vm, vm, vm],
             out_specs=(any_spec, any_spec, any_spec),
-            scratch_shapes=[dma((2 * L + 1,))],
+            scratch_shapes=[dma((2 * L * B + 1,))],
             compiler_params=pltpu.CompilerParams(vmem_limit_bytes=1 << 20),
             name="write_out",
         )(*outs)

time: 92.1 us -> 87.8 us (0.953)
  Pallas kernels: 90.5 us -> 86.1 us
    pallas_call x1, Pallas kernels: 84.4 us -> 79.1 us  [local_step(): pl.pallas_call(functools.partial(decode_kernel, cfg), out_shape=(pltpu.VM...]
    pallas_call x1, Pallas kernels: 6.03 us -> 7.05 us  [local_step(): pl.pallas_call(write_kernel, out_shape=(jax.ShapeDtypeStruct(cache_shape,...]
where the time goes in v5:
time: 87.8 us; the launch traced here: 87.6 us
  Pallas kernels  86.1 us (98%)
  between operations  1.47 us (2%)
    pallas_call x1, Pallas kernels, local_step(): pl.pallas_call(functools.partial(decode_kernel, cfg), out_shape=(pltpu.VM...  79.1 us
    pallas_call x1, Pallas kernels, local_step(): pl.pallas_call(write_kernel, out_shape=(jax.ShapeDtypeStruct(cache_shape,...  7.05 us

profile of v5, /device:TPU:0, one launch (start us, length us, event | category | flops | bytes accessed | tf_op | source)
XLA Modules:
  0.0 87.6 jit_solution(4125876570892983716)
XLA Ops:
  1.3 79.1 %decode_step.1 = (bf16[4,16,256,256]{3,2,1,0:T(8,128)(2,1)S(1)}, bf16[4,16,256,256]{3,2,1,0:T(8,128)(2,1)S(1)}, f32[16,8032]{1,0:T(8,128)S(1)}) custom-call(s32[2,32]{1,0:T(2,128)} %refs_0_.1, s32[1]{0:T(128)} %bitcast.16.refs_1_, bf16[16,1024]{1,0:T(8,128)(2,1)} %refs_2_.1, f32[1,16]{1,0:T(1,128)} %bitcast.21, f32[1,256]{1,0:T(1,128)} %constant.2.clone.refs_4_, ...), custom_call_target="tpu_custom_call" | custom-call | tf_op jit(solution)/shard_map/decode_step/pallas_call | solution.py:348
  80.4 7.0 %write_out.1 = (bf16[4,16,256,256]{3,2,1,0:T(8,128)(2,1)}, bf16[4,16,256,256]{3,2,1,0:T(8,128)(2,1)}, f32[16,8032]{1,0:T(8,128)}) custom-call(bf16[4,16,256,256]{3,2,1,0:T(8,128)(2,1)S(1)} %get-tuple-element.9.refs_0_, bf16[4,16,256,256]{3,2,1,0:T(8,128)(2,1)S(1)} %get-tuple-element.10.refs_1_, f32[16,8032]{1,0:T(8,128)S(1)} %get-tuple-element.11.refs_2_), custom_call_target="tpu_custom_call" | custom-call | tf_op jit(solution)/shard_map/write_out/pallas_call | solution.py:359

commit v6 on v5

--- a/solution.py
+++ b/solution.py
@@ -34,10 +34,11 @@
     L, B, D, HD, S, KH, FF, V, NM, SPAN = cfg
     (parent_ref, pos_ref, x_ref, score_ref, freq_ref, ga_ref, gm_ref, gf_ref,
      kc, vc, wq, wk, wv, wo, wg, wu, wd, wt, kst, vst, cand_ref,
-     kb0, kb1, vb0, vb1, wqb, wkb, wvb, wob, wgb, wub, wdb, ar, stat, scb, res, qs, lg, pr, osc, lgt,
-     sem_c, sem_w, sem_t, free, bsend, brecv, asend, arecv, ssend, srecv, csend, crecv) = refs
-    kb = (kb0, kb1)
-    vb = (vb0, vb1)
+     kb0, kb1, kb2, vb0, vb1, vb2, wqb, wkb, wvb, wob, wgb, wub, wdb, ar, stat, scb, xb, kn, vn, res, qs, lg, pr, osc, osend, orecv, lgt,
+     sem_c, sem_w, sem_t, free, bsend, brecv, asend, arecv, ssend, srecv, csend, crecv, xsend, xrecv, hsend, hrecv) = refs
+    slots = [0] + [1 + (l + 1) % 2 for l in range(1, L)]
+    kb = [(kb0, kb1, kb2)[j] for j in slots]
+    vb = [(vb0, vb1, vb2)[j] for j in slots]
     C = KH * HD
     NH, HB = res.shape[:2]
     me = lax.axis_index("model")
@@ -48,11 +49,11 @@
     own = pl.ds(spos * B, B)
 
     def cache_local(l):
-        return (pltpu.make_async_copy(kc.at[l], kb[l % 2].at[own], sem_c.at[2 * l]),
-                pltpu.make_async_copy(vc.at[l], vb[l % 2].at[own], sem_c.at[2 * l + 1]))
+        return (pltpu.make_async_copy(kc.at[l], kb[l].at[own], sem_c.at[2 * l]),
+                pltpu.make_async_copy(vc.at[l], vb[l].at[own], sem_c.at[2 * l + 1]))
 
     def cache_push(l):
-        return tuple(pltpu.make_async_remote_copy(src_ref=c.at[l], dst_ref=buf[l % 2].at[own], send_sem=bsend.at[2 * l + i],
+        return tuple(pltpu.make_async_remote_copy(src_ref=c.at[l], dst_ref=buf[l].at[own], send_sem=bsend.at[2 * l + i],
                                                   recv_sem=brecv.at[2 * l + i], device_id={"beam": partner}, device_id_type=MESH)
                      for i, (c, buf) in enumerate(((kc, kb), (vc, vb))))
 
@@ -62,7 +63,7 @@
         src, buf = weights[i]
         return pltpu.make_async_copy(src.at[l], buf.at[l % 2], sem_w.at[(l % 2) * 7 + i])
 
-    chunks = (kb0, vb0, kb1, vb1)
+    chunks = (kb1, vb1, kb2, vb2)
     NCH = D // S
     NT = lgt.shape[0]
     TN = lgt.shape[2]
@@ -85,9 +86,8 @@
 
     for i in range(3):
         weight(0, i).start()
-    for l in range(2):
-        for c in cache_local(l):
-            c.start()
+    for c in cache_local(0):
+        c.start()
 
     barrier = pltpu.get_barrier_semaphore()
     for k in range(1, NM):
@@ -100,19 +100,42 @@
     angle = pos.astype(F32) * freq_ref[...]
     cos = jnp.cos(angle)
     sin = jnp.sin(angle)
-    low = lax.rem(lax.broadcasted_iota(jnp.int32, (HB, C), 1), HD) < HD // 2
     rows = [lax.rem(parent_ref[sent, spos * B + b], SPAN * B) for b in range(B)]
+    near = [spos * B + lax.rem(r, B) for r in rows]
+    far = [spos * B + lax.rem(parent_ref[sent, (SPAN - 1 - spos) * B + b], B) for b in range(B)]
+
+    def rope(x):
+        low = lax.rem(lax.broadcasted_iota(jnp.int32, x.shape, 1), HD) < HD // 2
+        other = jnp.where(low, -pltpu.roll(x, C - HD // 2, 1), pltpu.roll(x, HD // 2, 1))
+        return x * cos + other * sin
+
+    def project(l, r):
+        ws = l % 2
+        h = rms(r, ga_ref[l:l + 1, :])
+        q = rope(dot(h, wqb[ws])).astype(BF16).astype(F32)
+        k = rope(dot(h, wkb[ws])).astype(BF16).astype(F32)
+        v = dot(h, wvb[ws]).astype(BF16).astype(F32)
+        return q * (HD ** -0.5), k, v
+
+    for j in range(3):
+        weight(0, j).wait()
+    own_q, own_k, own_v = project(0, x_ref[...].astype(F32))
+    kn[...] = own_k
+    vn[...] = own_v
 
     pl.semaphore_wait(barrier, NM)
 
     pushes = [cache_push(l) for l in range(L)]
-    for c in (pushes[0][0], pushes[0][1], pushes[1][0]):
-        c.start()
+    x_copy = pltpu.make_async_remote_copy(src_ref=x_ref, dst_ref=xb, send_sem=xsend, recv_sem=xrecv,
+                                          device_id={"beam": partner}, device_id_type=MESH)
+    x_copy.start()
     score_copy = pltpu.make_async_remote_copy(src_ref=scb.at[0], dst_ref=scb.at[1], send_sem=csend, recv_sem=crecv,
                                               device_id={"beam": partner}, device_id_type=MESH)
     score_copy.start()
     for i in range(3, 7):
         weight(0, i).start()
+    for c in cache_local(1):
+        c.start()
     for i in range(7):
         weight(1, i).start()
 
@@ -143,52 +166,89 @@
             total = total + ar[step * NM + k]
         return total
 
-    def rope(x):
-        other = jnp.where(low, -pltpu.roll(x, C - HD // 2, 1), pltpu.roll(x, HD // 2, 1))
-        return x * cos + other * sin
-
     head_of_lane = lax.broadcasted_iota(jnp.int32, (SUB, C), 1) // HD
     head_mask = head_of_lane == lax.broadcasted_iota(jnp.int32, (SUB, C), 0)
     here = lax.broadcasted_iota(jnp.int32, (C, S), 1) == pos
-    sends = [score_copy]
+    sends = [score_copy, x_copy]
     sends.extend(pushes[l][i] for l in range(L) for i in range(2))
 
-    def attend(l, i, r):
-        ws = l % 2
-        h = rms(r, ga_ref[l:l + 1, :])
-        if i == 0:
-            for j in range(3):
-                weight(l, j).wait()
-        q = rope(dot(h, wqb[ws])).astype(BF16).astype(F32)
-        k = rope(dot(h, wkb[ws])).astype(BF16).astype(F32)
-        v = dot(h, wvb[ws]).astype(BF16).astype(F32)
-        qs[i] = q * (HD ** -0.5)
-        pad = jnp.zeros((LANES - HB, C), F32)
-        k_cols = jnp.concatenate([k, pad], axis=0).T
-        v_cols = jnp.concatenate([v, pad], axis=0).T
-        if i == 0:
-            cache_local(l)[0].wait()
-            pushes[l][0].wait_recv()
+    def columns(x):
+        return jnp.concatenate([x, jnp.zeros((LANES - x.shape[0], C), F32)], axis=0).T
+
+    def insert(cols, b, row):
+        return jnp.where(here, jnp.broadcast_to(cols[:, b:b + 1], (C, S)).astype(BF16), row)
+
+    def attention(l, i, q, k, v, index, out, keep, ready):
+        qs[i] = q
+        k_cols = columns(k)
+        v_cols = columns(v)
+        ready(0)
         for b in range(HB):
-            kept = jnp.where(here, jnp.broadcast_to(k_cols[:, b:b + 1], (C, S)).astype(BF16), kb[ws][rows[i * HB + b]])
-            kst[l, i * HB + b] = kept
+            kept = insert(k_cols, b, kb[l][index[i * HB + b]])
+            if keep:
+                kst[l, i * HB + b] = kept
             qb = jnp.where(head_mask, jnp.broadcast_to(qs[i, b:b + 1, :], (SUB, C)), 0.0).astype(BF16)
             lg[i, b * SUB:(b + 1) * SUB, :] = dot(qb, kept)
         logits = lg[i]
         logits = jnp.where(lax.broadcasted_iota(jnp.int32, logits.shape, 1) <= pos, logits, -jnp.inf)
         e = jnp.exp(logits - jnp.max(logits, axis=-1, keepdims=True))
         pr[i] = e / jnp.sum(e, axis=-1, keepdims=True)
-        if i == 0:
-            cache_local(l)[1].wait()
-            pushes[l][1].wait_recv()
+        ready(1)
         for b in range(HB):
-            kept = jnp.where(here, jnp.broadcast_to(v_cols[:, b:b + 1], (C, S)).astype(BF16), vb[ws][rows[i * HB + b]])
-            vst[l, i * HB + b] = kept
+            kept = insert(v_cols, b, vb[l][index[i * HB + b]])
+            if keep:
+                vst[l, i * HB + b] = kept
             ob = dot_t(pr[i, b * SUB:(b + 1) * SUB, :].astype(BF16), kept)
-            osc[i, b:b + 1, :] = jnp.sum(jnp.where(head_mask, ob, 0.0), axis=0, keepdims=True)
+            out[i, b:b + 1, :] = jnp.sum(jnp.where(head_mask, ob, 0.0), axis=0, keepdims=True)
+
+    def project_out(l, i, o):
         if i == 0:
             weight(l, 3).wait()
-        return reduce_start(2 * l * NH + i, dot(osc[i].astype(BF16), wob[ws]))
+        return reduce_start(2 * l * NH + i, dot(o.astype(BF16), wob[l % 2]))
+
+    def attend(l, i, r):
+        if i == 0:
+            for j in range(3):
+                weight(l, j).wait()
+        q, k, v = project(l, r)
+
+        def ready(which):
+            if i == 0:
+                cache_local(l)[which].wait()
+                pushes[l][which].wait_recv()
+
+        attention(l, i, q, k, v, rows, osc, True, ready)
+        return project_out(l, i, osc[i])
+
+    def attend_first():
+        for c in cache_local(0):
+            c.wait()
+        part = lambda x, i: x[i * HB:(i + 1) * HB, :]
+        for i in range(NH):
+            attention(0, i, part(own_q, i), part(own_k, i), part(own_v, i), near, osc, False, lambda w: None)
+        x_copy.wait_recv()
+        q, k, v = project(0, xb[...].astype(F32))
+        copies = []
+        for i in range(NH):
+            attention(0, i, part(q, i), part(k, i), part(v, i), far, osend, False, lambda w: None)
+            copies.append(pltpu.make_async_remote_copy(src_ref=osend.at[i], dst_ref=orecv.at[i], send_sem=hsend.at[i], recv_sem=hrecv.at[i],
+                                                       device_id={"beam": partner}, device_id_type=MESH))
+            copies[i].start()
+        sends.extend(copies)
+        steps = []
+        for i in range(NH):
+            copies[i].wait_recv()
+            home = jnp.zeros((HB, C), jnp.int32)
+            for b in range(HB):
+                home = jnp.where(lax.broadcasted_iota(jnp.int32, (HB, C), 0) == b, lax.div(rows[i * HB + b], B), home)
+            steps.append(project_out(0, i, jnp.where(home == spos, osc[i], orecv[i])))
+        return steps
+
+    def keep_first(which):
+        cols = columns((kn, vn)[which][...])
+        pushes[0][which].wait_recv()
+        for b in range(B):
+            (kst, vst)[which][0, b] = insert(cols, b, (kb, vb)[which][0][rows[b]])
 
     def mlp(l, i, r):
         ws = l % 2
@@ -205,31 +265,38 @@
 
     for i in range(NH):
         res[i] = x_ref[i * HB:(i + 1) * HB, :].astype(F32)
-    started = [None] * NH
+    started = attend_first()
+    order = [(1, 0), (1, 1)] + [(l, w) for l in range(2, L) for w in range(2)] + [(0, 0), (0, 1)]
+    order = [order[:2]] + [[o] for o in order[2:]]
     for l in range(L):
-        for i in range(NH):
-            if l > 0:
+        if l > 0:
+            for i in range(NH):
                 res[i] = res[i] + reduce_finish(started[i])
-            started[i] = attend(l, i, res[i])
+                started[i] = attend(l, i, res[i])
+            if l + 2 < L:
+                pl.semaphore_signal(free, inc=1, device_id={"beam": partner}, device_id_type=MESH)
+        for o in order[2 * l] if 2 * l < len(order) else []:
+            pushes[o[0]][o[1]].start()
         if l + 2 < L:
-            pl.semaphore_signal(free, inc=1, device_id={"beam": partner}, device_id_type=MESH)
             for c in cache_local(l + 2):
                 c.start()
-        if l + 1 < L:
-            pushes[l + 1][1].start()
-        if l + 2 < L:
             for j in range(4):
                 weight(l + 2, j).start()
         if l == L - 1:
             vocab_all(range(NCH), lambda c: c.start())
+            keep_first(0)
         for i in range(NH):
             res[i] = res[i] + reduce_finish(started[i])
             started[i] = mlp(l, i, res[i])
+        for o in order[2 * l + 1] if 2 * l + 1 < len(order) else []:
+            if o[0] >= 3 and o[1] == 0:
+                pl.semaphore_wait(free, 1)
+            pushes[o[0]][o[1]].start()
         if l + 2 < L:
-            pl.semaphore_wait(free, 1)
-            pushes[l + 2][0].start()
             for j in range(4, 7):
                 weight(l + 2, j).start()
+        if l == L - 1:
+            keep_first(1)
     for i in range(NH):
         res[i] = res[i] + reduce_finish(started[i])
 
@@ -292,7 +359,7 @@
     for i in range(n):
         src, dst = refs[i], refs[n + i]
         if len(src.shape) > 2:
-            copies += [(src.at[j, k], dst.at[j, k]) for j in range(src.shape[0]) for k in range(src.shape[1])]
+            copies += [(src.at[j], dst.at[j]) for j in range(src.shape[0])]
         else:
             copies.append((src, dst))
     copies = [pltpu.make_async_copy(a, b, sem.at[j]) for j, (a, b) in enumerate(copies)]
@@ -335,15 +402,16 @@
         NT = -(-V // TN)
         dma = pltpu.SemaphoreType.DMA
         cache_shape = (L, B, C, S)
-        scratch = ([pltpu.VMEM((span * B, C, S), BF16) for _ in range(4)]
+        scratch = ([pltpu.VMEM((span * B, C, S), BF16) for _ in range(6)]
                    + [pltpu.VMEM((2, D, C), BF16)] * 3 + [pltpu.VMEM((2, C, D), BF16)]
                    + [pltpu.VMEM((2, D, FF), BF16)] * 2 + [pltpu.VMEM((2, FF, D), BF16)]
                    + [pltpu.VMEM((steps * NH * n_model, HB, D), F32), pltpu.VMEM((n_model, 2, B, LANES), F32), pltpu.VMEM((2, SUB, LANES), F32),
+                      pltpu.VMEM((B, D), BF16), pltpu.VMEM((B, C), F32), pltpu.VMEM((B, C), F32),
                       pltpu.VMEM((NH, HB, D), F32), pltpu.VMEM((NH, HB, C), F32), pltpu.VMEM((NH, HB * SUB, S), F32),
-                      pltpu.VMEM((NH, HB * SUB, S), F32), pltpu.VMEM((NH, HB, C), F32), pltpu.VMEM((NT, B, TN), F32),
+                      pltpu.VMEM((NH, HB * SUB, S), F32)] + [pltpu.VMEM((NH, HB, C), F32)] * 3 + [ pltpu.VMEM((NT, B, TN), F32),
                       dma((2 * L,)), dma((14,)), dma((D // S * NT,)), pltpu.SemaphoreType.REGULAR, dma((2 * L,)), dma((2 * L,)),
                       dma((steps * NH * (n_model - 1),)), dma((steps * NH * n_model,)), dma((n_model - 1,)), dma((n_model - 1,)),
-                      dma, dma])
+                      dma, dma, dma, dma, dma((NH,)), dma((NH,))])
         limit = 64 * 1024 * 1024 - 65536
         outs = pl.pallas_call(
             functools.partial(decode_kernel, cfg),
@@ -362,7 +430,7 @@
                        jax.ShapeDtypeStruct((B, V), F32)),
             in_specs=[vm, vm, vm],
             out_specs=(any_spec, any_spec, any_spec),
-            scratch_shapes=[dma((2 * L * B + 1,))],
+            scratch_shapes=[dma((2 * L + 1,))],
             compiler_params=pltpu.CompilerParams(vmem_limit_bytes=1 << 20),
             name="write_out",
         )(*outs)

time: 87.8 us -> 85.9 us (0.978)
  Pallas kernels: 86.1 us -> 84.3 us
    pallas_call x1, Pallas kernels: 7.05 us -> 6.03 us  [local_step(): pl.pallas_call(write_kernel, out_shape=(jax.ShapeDtypeStruct(cache_shape,...]
where the time goes in v6:
time: 85.9 us; the launch traced here: 85.7 us
  Pallas kernels  84.3 us (98%)
  between operations  1.47 us (2%)
    pallas_call x1, Pallas kernels, local_step(): pl.pallas_call(functools.partial(decode_kernel, cfg), out_shape=(pltpu.VM...  78.2 us
    pallas_call x1, Pallas kernels, local_step(): pl.pallas_call(write_kernel, out_shape=(jax.ShapeDtypeStruct(cache_shape,...  6.03 us

profile of v6, /device:TPU:0, one launch (start us, length us, event | category | flops | bytes accessed | tf_op | source)
XLA Modules:
  0.0 85.7 jit_solution(1687126041167636466)
XLA Ops:
  1.3 78.2 %decode_step.1 = (bf16[4,16,256,256]{3,2,1,0:T(8,128)(2,1)S(1)}, bf16[4,16,256,256]{3,2,1,0:T(8,128)(2,1)S(1)}, f32[16,8032]{1,0:T(8,128)S(1)}) custom-call(s32[2,32]{1,0:T(2,128)} %refs_0_.1, s32[1]{0:T(128)} %bitcast.16.refs_1_, bf16[16,1024]{1,0:T(8,128)(2,1)} %refs_2_.1, f32[1,16]{1,0:T(1,128)} %bitcast.21, f32[1,256]{1,0:T(1,128)} %constant.2.clone.refs_4_, ...), custom_call_target="tpu_custom_call" | custom-call | tf_op jit(solution)/shard_map/decode_step/pallas_call | solution.py:416
  79.5 6.0 %write_out.1 = (bf16[4,16,256,256]{3,2,1,0:T(8,128)(2,1)}, bf16[4,16,256,256]{3,2,1,0:T(8,128)(2,1)}, f32[16,8032]{1,0:T(8,128)}) custom-call(bf16[4,16,256,256]{3,2,1,0:T(8,128)(2,1)S(1)} %get-tuple-element.9.refs_0_, bf16[4,16,256,256]{3,2,1,0:T(8,128)(2,1)S(1)} %get-tuple-element.10.refs_1_, f32[16,8032]{1,0:T(8,128)S(1)} %get-tuple-element.11.refs_2_), custom_call_target="tpu_custom_call" | custom-call | tf_op jit(solution)/shard_map/write_out/pallas_call | solution.py:427

commit v7 on v6

--- a/solution.py
+++ b/solution.py
@@ -53,9 +53,9 @@
                 pltpu.make_async_copy(vc.at[l], vb[l].at[own], sem_c.at[2 * l + 1]))
 
     def cache_push(l):
-        return tuple(pltpu.make_async_remote_copy(src_ref=c.at[l], dst_ref=buf[l].at[own], send_sem=bsend.at[2 * l + i],
+        return tuple(pltpu.make_async_remote_copy(src_ref=buf[l].at[own], dst_ref=buf[l].at[own], send_sem=bsend.at[2 * l + i],
                                                   recv_sem=brecv.at[2 * l + i], device_id={"beam": partner}, device_id_type=MESH)
-                     for i, (c, buf) in enumerate(((kc, kb), (vc, vb))))
+                     for i, buf in enumerate((kb, vb)))
 
     weights = ((wq, wqb), (wk, wkb), (wv, wvb), (wo, wob), (wg, wgb), (wu, wub), (wd, wdb))
 
@@ -170,7 +170,6 @@
     head_mask = head_of_lane == lax.broadcasted_iota(jnp.int32, (SUB, C), 0)
     here = lax.broadcasted_iota(jnp.int32, (C, S), 1) == pos
     sends = [score_copy, x_copy]
-    sends.extend(pushes[l][i] for l in range(L) for i in range(2))
 
     def columns(x):
         return jnp.concatenate([x, jnp.zeros((LANES - x.shape[0], C), F32)], axis=0).T
@@ -214,7 +213,6 @@
 
         def ready(which):
             if i == 0:
-                cache_local(l)[which].wait()
                 pushes[l][which].wait_recv()
 
         attention(l, i, q, k, v, rows, osc, True, ready)
@@ -265,6 +263,11 @@
 
     for i in range(NH):
         res[i] = x_ref[i * HB:(i + 1) * HB, :].astype(F32)
+    def push(l, which):
+        if l > 0:
+            cache_local(l)[which].wait()
+        pushes[l][which].start()
+
     started = attend_first()
     order = [(1, 0), (1, 1)] + [(l, w) for l in range(2, L) for w in range(2)] + [(0, 0), (0, 1)]
     order = [order[:2]] + [[o] for o in order[2:]]
@@ -276,13 +279,18 @@
             if l + 2 < L:
                 pl.semaphore_signal(free, inc=1, device_id={"beam": partner}, device_id_type=MESH)
         for o in order[2 * l] if 2 * l < len(order) else []:
-            pushes[o[0]][o[1]].start()
+            push(*o)
         if l + 2 < L:
-            for c in cache_local(l + 2):
-                c.start()
+            for which in range(2):
+                if l > 0:
+                    pushes[l][which].wait_send()
+                cache_local(l + 2)[which].start()
             for j in range(4):
                 weight(l + 2, j).start()
         if l == L - 1:
+            for j in (l - 1, l):
+                for which in range(2):
+                    pushes[j][which].wait_send()
             vocab_all(range(NCH), lambda c: c.start())
             keep_first(0)
         for i in range(NH):
@@ -291,7 +299,7 @@
         for o in order[2 * l + 1] if 2 * l + 1 < len(order) else []:
             if o[0] >= 3 and o[1] == 0:
                 pl.semaphore_wait(free, 1)
-            pushes[o[0]][o[1]].start()
+            push(*o)
         if l + 2 < L:
             for j in range(4, 7):
                 weight(l + 2, j).start()
@@ -348,6 +356,7 @@
     for n in range(NT):
         hi = min((n + 1) * TN, V)
         cand_ref[:, n * TN:hi] = parent_score + ((lgt[n] - gm) - log_s)[:, :hi - n * TN]
+    sends.extend(pushes[0])
     for c in sends:
         c.wait_send()
 

time: 85.9 us -> 85.2 us (level)
  no operation moved by 1% of the time
where the time goes in v7:
time: 85.2 us; the launch traced here: 85 us
  Pallas kernels  83.6 us (98%)
  between operations  1.47 us (2%)
    pallas_call x1, Pallas kernels, local_step(): pl.pallas_call(functools.partial(decode_kernel, cfg), out_shape=(pltpu.VM...  77.5 us
    pallas_call x1, Pallas kernels, local_step(): pl.pallas_call(write_kernel, out_shape=(jax.ShapeDtypeStruct(cache_shape,...  6.03 us

profile of v7, /device:TPU:0, one launch (start us, length us, event | category | flops | bytes accessed | tf_op | source)
XLA Modules:
  0.0 85.0 jit_solution(1932642202726395823)
XLA Ops:
  1.3 77.5 %decode_step.1 = (bf16[4,16,256,256]{3,2,1,0:T(8,128)(2,1)S(1)}, bf16[4,16,256,256]{3,2,1,0:T(8,128)(2,1)S(1)}, f32[16,8032]{1,0:T(8,128)S(1)}) custom-call(s32[2,32]{1,0:T(2,128)} %refs_0_.1, s32[1]{0:T(128)} %bitcast.16.refs_1_, bf16[16,1024]{1,0:T(8,128)(2,1)} %refs_2_.1, f32[1,16]{1,0:T(1,128)} %bitcast.21, f32[1,256]{1,0:T(1,128)} %constant.2.clone.refs_4_, ...), custom_call_target="tpu_custom_call" | custom-call | tf_op jit(solution)/shard_map/decode_step/pallas_call | solution.py:425
  78.8 6.0 %write_out.1 = (bf16[4,16,256,256]{3,2,1,0:T(8,128)(2,1)}, bf16[4,16,256,256]{3,2,1,0:T(8,128)(2,1)}, f32[16,8032]{1,0:T(8,128)}) custom-call(bf16[4,16,256,256]{3,2,1,0:T(8,128)(2,1)S(1)} %get-tuple-element.9.refs_0_, bf16[4,16,256,256]{3,2,1,0:T(8,128)(2,1)S(1)} %get-tuple-element.10.refs_1_, f32[16,8032]{1,0:T(8,128)S(1)} %get-tuple-element.11.refs_2_), custom_call_target="tpu_custom_call" | custom-call | tf_op jit(solution)/shard_map/write_out/pallas_call | solution.py:436

commit v8 on v7

--- a/solution.py
+++ b/solution.py
@@ -405,7 +405,7 @@
         vm = pl.BlockSpec(memory_space=pltpu.VMEM)
         sm = pl.BlockSpec(memory_space=pltpu.SMEM)
         steps = 2 * L
-        NH = 4
+        NH = 2
         HB = B // NH
         TN = C
         NT = -(-V // TN)

time: 85.2 us -> 87.2 us (1.023)
  Pallas kernels: 83.6 us -> 85.6 us
    pallas_call x1, Pallas kernels: 77.5 us -> 79.6 us  [local_step(): pl.pallas_call(functools.partial(decode_kernel, cfg), out_shape=(pltpu.VM...]
where the time goes in v8:
time: 87.2 us; the launch traced here: 87 us
  Pallas kernels  85.6 us (98%)
  between operations  1.45 us (2%)
    pallas_call x1, Pallas kernels, local_step(): pl.pallas_call(functools.partial(decode_kernel, cfg), out_shape=(pltpu.VM...  79.6 us
    pallas_call x1, Pallas kernels, local_step(): pl.pallas_call(write_kernel, out_shape=(jax.ShapeDtypeStruct(cache_shape,...  6.03 us

profile of v8, /device:TPU:0, one launch (start us, length us, event | category | flops | bytes accessed | tf_op | source)
XLA Modules:
  0.0 87.0 jit_solution(16578021000156432497)
XLA Ops:
  1.3 79.6 %decode_step.1 = (bf16[4,16,256,256]{3,2,1,0:T(8,128)(2,1)S(1)}, bf16[4,16,256,256]{3,2,1,0:T(8,128)(2,1)S(1)}, f32[16,8032]{1,0:T(8,128)S(1)}) custom-call(s32[2,32]{1,0:T(2,128)} %refs_0_.1, s32[1]{0:T(128)} %bitcast.16.refs_1_, bf16[16,1024]{1,0:T(8,128)(2,1)} %refs_2_.1, f32[1,16]{1,0:T(1,128)} %bitcast.21, f32[1,256]{1,0:T(1,128)} %constant.2.clone.refs_4_, ...), custom_call_target="tpu_custom_call" | custom-call | tf_op jit(solution)/shard_map/decode_step/pallas_call | solution.py:425
  80.8 6.0 %write_out.1 = (bf16[4,16,256,256]{3,2,1,0:T(8,128)(2,1)}, bf16[4,16,256,256]{3,2,1,0:T(8,128)(2,1)}, f32[16,8032]{1,0:T(8,128)}) custom-call(bf16[4,16,256,256]{3,2,1,0:T(8,128)(2,1)S(1)} %get-tuple-element.9.refs_0_, bf16[4,16,256,256]{3,2,1,0:T(8,128)(2,1)S(1)} %get-tuple-element.10.refs_1_, f32[16,8032]{1,0:T(8,128)S(1)} %get-tuple-element.11.refs_2_), custom_call_target="tpu_custom_call" | custom-call | tf_op jit(solution)/shard_map/write_out/pallas_call | solution.py:436

commit v9 on v7

--- a/solution.py
+++ b/solution.py
@@ -41,6 +41,7 @@
     vb = [(vb0, vb1, vb2)[j] for j in slots]
     C = KH * HD
     NH, HB = res.shape[:2]
+    NP = bsend.shape[0] // (2 * L)
     me = lax.axis_index("model")
     beam = lax.axis_index("beam")
     spos = lax.rem(beam, SPAN)
@@ -52,10 +53,11 @@
         return (pltpu.make_async_copy(kc.at[l], kb[l].at[own], sem_c.at[2 * l]),
                 pltpu.make_async_copy(vc.at[l], vb[l].at[own], sem_c.at[2 * l + 1]))
 
-    def cache_push(l):
-        return tuple(pltpu.make_async_remote_copy(src_ref=buf[l].at[own], dst_ref=buf[l].at[own], send_sem=bsend.at[2 * l + i],
-                                                  recv_sem=brecv.at[2 * l + i], device_id={"beam": partner}, device_id_type=MESH)
-                     for i, buf in enumerate((kb, vb)))
+    def cache_push(l, which, j):
+        buf = (kb, vb)[which][l].at[pl.ds(spos * B + j * (B // NP), B // NP)]
+        n = (2 * l + which) * NP + j
+        return pltpu.make_async_remote_copy(src_ref=buf, dst_ref=buf, send_sem=bsend.at[n], recv_sem=brecv.at[n],
+                                            device_id={"beam": partner}, device_id_type=MESH)
 
     weights = ((wq, wqb), (wk, wkb), (wv, wvb), (wo, wob), (wg, wgb), (wu, wub), (wd, wdb))
 
@@ -125,7 +127,7 @@
 
     pl.semaphore_wait(barrier, NM)
 
-    pushes = [cache_push(l) for l in range(L)]
+    pushes = [[[cache_push(l, which, j) for j in range(NP)] for which in range(2)] for l in range(L)]
     x_copy = pltpu.make_async_remote_copy(src_ref=x_ref, dst_ref=xb, send_sem=xsend, recv_sem=xrecv,
                                           device_id={"beam": partner}, device_id_type=MESH)
     x_copy.start()
@@ -213,7 +215,8 @@
 
         def ready(which):
             if i == 0:
-                pushes[l][which].wait_recv()
+                for c in pushes[l][which]:
+                    c.wait_recv()
 
         attention(l, i, q, k, v, rows, osc, True, ready)
         return project_out(l, i, osc[i])
@@ -244,7 +247,8 @@
 
     def keep_first(which):
         cols = columns((kn, vn)[which][...])
-        pushes[0][which].wait_recv()
+        for c in pushes[0][which]:
+            c.wait_recv()
         for b in range(B):
             (kst, vst)[which][0, b] = insert(cols, b, (kb, vb)[which][0][rows[b]])
 
@@ -263,47 +267,52 @@
 
     for i in range(NH):
         res[i] = x_ref[i * HB:(i + 1) * HB, :].astype(F32)
-    def push(l, which):
-        if l > 0:
-            cache_local(l)[which].wait()
-        pushes[l][which].start()
+    queue = [(l, which, j) for l in list(range(1, L)) + [0] for which in range(2) for j in range(NP)]
+
+    def feed(count):
+        for _ in range(min(count, len(queue))):
+            l, which, j = queue.pop(0)
+            if j == 0 and l > 0:
+                if l >= 3 and which == 0:
+                    pl.semaphore_wait(free, 1)
+                cache_local(l)[which].wait()
+            pushes[l][which][j].start()
 
     started = attend_first()
-    order = [(1, 0), (1, 1)] + [(l, w) for l in range(2, L) for w in range(2)] + [(0, 0), (0, 1)]
-    order = [order[:2]] + [[o] for o in order[2:]]
     for l in range(L):
         if l > 0:
             for i in range(NH):
                 res[i] = res[i] + reduce_finish(started[i])
                 started[i] = attend(l, i, res[i])
+                feed(NP // NH)
             if l + 2 < L:
                 pl.semaphore_signal(free, inc=1, device_id={"beam": partner}, device_id_type=MESH)
-        for o in order[2 * l] if 2 * l < len(order) else []:
-            push(*o)
+        else:
+            feed(NP + NP // 2)
         if l + 2 < L:
             for which in range(2):
                 if l > 0:
-                    pushes[l][which].wait_send()
+                    for c in pushes[l][which]:
+                        c.wait_send()
                 cache_local(l + 2)[which].start()
             for j in range(4):
                 weight(l + 2, j).start()
         if l == L - 1:
             for j in (l - 1, l):
                 for which in range(2):
-                    pushes[j][which].wait_send()
+                    for c in pushes[j][which]:
+                        c.wait_send()
             vocab_all(range(NCH), lambda c: c.start())
             keep_first(0)
         for i in range(NH):
             res[i] = res[i] + reduce_finish(started[i])
             started[i] = mlp(l, i, res[i])
-        for o in order[2 * l + 1] if 2 * l + 1 < len(order) else []:
-            if o[0] >= 3 and o[1] == 0:
-                pl.semaphore_wait(free, 1)
-            push(*o)
+            feed(NP // NH)
         if l + 2 < L:
             for j in range(4, 7):
                 weight(l + 2, j).start()
         if l == L - 1:
+            feed(len(queue))
             keep_first(1)
     for i in range(NH):
         res[i] = res[i] + reduce_finish(started[i])
@@ -356,7 +365,7 @@
     for n in range(NT):
         hi = min((n + 1) * TN, V)
         cand_ref[:, n * TN:hi] = parent_score + ((lgt[n] - gm) - log_s)[:, :hi - n * TN]
-    sends.extend(pushes[0])
+    sends.extend(pushes[0][0] + pushes[0][1])
     for c in sends:
         c.wait_send()
 
@@ -406,6 +415,7 @@
         sm = pl.BlockSpec(memory_space=pltpu.SMEM)
         steps = 2 * L
         NH = 4
+        NP = 4
         HB = B // NH
         TN = C
         NT = -(-V // TN)
@@ -418,7 +428,7 @@
                       pltpu.VMEM((B, D), BF16), pltpu.VMEM((B, C), F32), pltpu.VMEM((B, C), F32),
                       pltpu.VMEM((NH, HB, D), F32), pltpu.VMEM((NH, HB, C), F32), pltpu.VMEM((NH, HB * SUB, S), F32),
                       pltpu.VMEM((NH, HB * SUB, S), F32)] + [pltpu.VMEM((NH, HB, C), F32)] * 3 + [ pltpu.VMEM((NT, B, TN), F32),
-                      dma((2 * L,)), dma((14,)), dma((D // S * NT,)), pltpu.SemaphoreType.REGULAR, dma((2 * L,)), dma((2 * L,)),
+                      dma((2 * L,)), dma((14,)), dma((D // S * NT,)), pltpu.SemaphoreType.REGULAR, dma((2 * L * NP,)), dma((2 * L * NP,)),
                       dma((steps * NH * (n_model - 1),)), dma((steps * NH * n_model,)), dma((n_model - 1,)), dma((n_model - 1,)),
                       dma, dma, dma, dma, dma((NH,)), dma((NH,))])
         limit = 64 * 1024 * 1024 - 65536

time: 85.2 us -> 87.4 us (1.026)
  Pallas kernels: 83.6 us -> 85.8 us
    pallas_call x1, Pallas kernels: 77.5 us -> 79.7 us  [local_step(): pl.pallas_call(functools.partial(decode_kernel, cfg), out_shape=(pltpu.VM...]
where the time goes in v9:
time: 87.4 us; the launch traced here: 87.2 us
  Pallas kernels  85.8 us (98%)
  between operations  1.47 us (2%)
    pallas_call x1, Pallas kernels, local_step(): pl.pallas_call(functools.partial(decode_kernel, cfg), out_shape=(pltpu.VM...  79.7 us
    pallas_call x1, Pallas kernels, local_step(): pl.pallas_call(write_kernel, out_shape=(jax.ShapeDtypeStruct(cache_shape,...  6.03 us

profile of v9, /device:TPU:0, one launch (start us, length us, event | category | flops | bytes accessed | tf_op | source)
XLA Modules:
  0.0 87.2 jit_solution(7964690737038168740)
XLA Ops:
  1.3 79.7 %decode_step.1 = (bf16[4,16,256,256]{3,2,1,0:T(8,128)(2,1)S(1)}, bf16[4,16,256,256]{3,2,1,0:T(8,128)(2,1)S(1)}, f32[16,8032]{1,0:T(8,128)S(1)}) custom-call(s32[2,32]{1,0:T(2,128)} %refs_0_.1, s32[1]{0:T(128)} %bitcast.16.refs_1_, bf16[16,1024]{1,0:T(8,128)(2,1)} %refs_2_.1, f32[1,16]{1,0:T(1,128)} %bitcast.21, f32[1,256]{1,0:T(1,128)} %constant.2.clone.refs_4_, ...), custom_call_target="tpu_custom_call" | custom-call | tf_op jit(solution)/shard_map/decode_step/pallas_call | solution.py:435
  81.0 6.0 %write_out.1 = (bf16[4,16,256,256]{3,2,1,0:T(8,128)(2,1)}, bf16[4,16,256,256]{3,2,1,0:T(8,128)(2,1)}, f32[16,8032]{1,0:T(8,128)}) custom-call(bf16[4,16,256,256]{3,2,1,0:T(8,128)(2,1)S(1)} %get-tuple-element.9.refs_0_, bf16[4,16,256,256]{3,2,1,0:T(8,128)(2,1)S(1)} %get-tuple-element.10.refs_1_, f32[16,8032]{1,0:T(8,128)S(1)} %get-tuple-element.11.refs_2_), custom_call_target="tpu_custom_call" | custom-call | tf_op jit(solution)/shard_map/write_out/pallas_call | solution.py:446
